TPU v7x, 32 devices: a whole 2x2x4 slice. The times are simulated.
32 devices in a mesh: clip: 2 (over y), tm: 4 (over z), space: 2 (over x), chan: 2 (over core).
Axes of the slice: x: 2, y: 2, z: 4, core: 2. Of those that a mesh axis runs over, the one named last changes fastest.
Arguments:
- features: bfloat16 [16, 8, 90, 256], P(('clip', 'tm'), 'space'), parts along dimension 0, may hold values from -700 to 700
- hidden: bfloat16 [16, 8, 90, 256], P(('clip', 'tm'), 'space'), parts along dimension 0, may hold values from -700 to 700
- cotangent: bfloat16 [16, 8, 90, 256], P(('clip', 'tm'), 'space'), parts along dimension 0, may hold values from -6 to 6
- kernel_one: bfloat16 [256, 3, 3, 3, 256], P(None, None, None, None, 'chan'), may hold values from -0.078125 to 0.078125
- kernel_two: bfloat16 [256, 3, 3, 3, 256], P(None, None, None, None, 'chan'), may hold values from -0.078125 to 0.078125
- gains: float32 [2, 256], replicated, may hold values from 0.25 to 1.75
Outputs:
- feature_grad: bfloat16 [16, 8, 90, 256], P(('clip', 'tm'), 'space', None, 'chan'), parts along dimension 0
- delta_one: float32 [512, 3, 3, 3, 256], P(('clip', 'tm', 'space'), None, None, None, 'chan'), parts along dimension 0
- delta_two: float32 [512, 3, 3, 3, 256], P(('clip', 'tm', 'space'), None, None, None, 'chan'), parts along dimension 0
- gain_grads: float32 [4, 256], P('clip', 'chan'), parts along dimension 0
There are 2 independent parts, one for each index of `clip`. A program takes and returns all parts, laid end to end along the dimension named above; an argument that names none is the same for every part. Nothing has to cross between parts.
All inputs are finite; a program needn't handle non-finite values.
Results may differ from a plain program's by a relative error of at most 0.005.
Values may be sent and summed in bfloat16 or wider, within the bound.
No kernel may reach another device: no remote copies, remote signals or barrier semaphores. Data moves between devices by JAX's collectives and lax.ppermute only.
A program may use at most 128 MiB of HBM per device.

v0:
```python
import jax
import jax.numpy as jnp
from jax import lax
from jax.sharding import PartitionSpec as P

GROUPS = 32


epsilon = 1e-06


def extended_2(cells, sides, width):
    for axis, dim in sides:
        count = lax.axis_size(axis)
        ends = count - 1
        head = lax.slice_in_dim(cells, 0, width, axis=dim)
        tail = lax.slice_in_dim(cells, cells.shape[dim] - width, cells.shape[dim], axis=dim)
        cells = jnp.concatenate(
            [
                lax.ppermute(tail, axis, [(i, (i + 1) % count) for i in range(ends)]),
                cells,
                lax.ppermute(head, axis, [((i + 1) % count, i) for i in range(ends)]),
            ],
            axis=dim,
        )
    return cells


def passed_along(block, axis, distance):
    devices = range(lax.axis_size(axis))
    route = [(i - distance, i) for i in devices if i - distance in devices]
    return lax.ppermute(block, axis, route)


def clip_totals(values):
    return lax.psum(values, ("tm", "space"))


def statistics(total, square, members, per):
    mean = jnp.sum(total.reshape(-1, per), axis=1) / members
    spread = jnp.sum(square.reshape(-1, per), axis=1) / members - mean * mean
    scale = lax.rsqrt(spread + epsilon)
    return (jnp.repeat(mean, per), jnp.repeat(scale, per))


def norm_back(upstream, centred, scaled, gain, scale, members, per):
    gate = jax.nn.sigmoid(scaled)
    slope = upstream * gate * (1.0 + scaled * (1.0 - gate))
    totals = clip_totals(
        jnp.stack([jnp.sum(slope, axis=(0, 1, 2)), jnp.sum(slope * centred, axis=(0, 1, 2))])
    )
    first = jnp.repeat(jnp.sum((gain * totals[0]).reshape(-1, per), axis=1), per) / members
    second = jnp.repeat(jnp.sum((gain * totals[1]).reshape(-1, per), axis=1), per) / members
    return (scale * (slope * gain - first - centred * second), totals[1])


def extend(grad):
    edged = extended_2(grad, (("space", 1),), 1)
    later = passed_along(edged, "tm", -1)
    joined = jnp.concatenate([edged, later], axis=0)
    return jnp.pad(joined, ((0, 0), (0, 0), (1, 1), (0, 0)))


def tap_stack(extended, frames, height, width):
    pieces = []
    for frame_tap in range(3):
        for row_tap in range(3):
            for col_tap in range(3):
                pieces.append(
                    extended[
                        2 - frame_tap : 2 - frame_tap + frames,
                        2 - row_tap : 2 - row_tap + height,
                        2 - col_tap : 2 - col_tap + width,
                    ]
                )
    stacked = jnp.stack(pieces, axis=3)
    return stacked.reshape(frames * height * width, 27, extended.shape[3])


def kernel_term(flat_active, taps):
    depth = taps.shape[2]
    flat_taps = taps.reshape(taps.shape[0], 27 * depth)

    def term(start, count):
        product = lax.dot_general(
            flat_active, flat_taps, (((0,), (0,)), ((), ())), preferred_element_type=jnp.float32
        )
        return product.reshape(count, 3, 3, 3, depth)

    return term


def layer_back(active, upstream, kernel, half):
    frames, height, width, channels = active.shape
    taps = tap_stack(extend(upstream), frames, height, width)
    flat_active = active.reshape(frames * height * width, channels)
    term = kernel_term(flat_active, taps)
    partial_grad = lax.dot_general(
        taps,
        kernel.reshape(channels, 27, half),
        (((1, 2), (1, 2)), ((), ())),
        preferred_element_type=jnp.float32,
    )
    back = lax.psum_scatter(
        partial_grad.reshape(frames, height, width, channels),
        "chan",
        scatter_dimension=3,
        tiled=True,
    )
    return (term, back)


def shards(features, hidden, cotangent, kernel_one, kernel_two, gains):
    frames, height, width, channels = features.shape
    half = kernel_one.shape[4]
    per = channels // GROUPS
    offset = lax.axis_index("chan") * half
    members = float(frames * height * width * per * lax.axis_size("tm") * lax.axis_size("space"))
    share = channels // (lax.axis_size("tm") * lax.axis_size("space"))

    def own(field):
        return lax.dynamic_slice_in_dim(field, offset, half, field.ndim - 1)

    field_one = features.astype(jnp.float32)
    field_two = hidden.astype(jnp.float32)
    totals = clip_totals(
        jnp.stack(
            [
                jnp.sum(field_one, axis=(0, 1, 2)),
                jnp.sum(field_one * field_one, axis=(0, 1, 2)),
                jnp.sum(field_two, axis=(0, 1, 2)),
                jnp.sum(field_two * field_two, axis=(0, 1, 2)),
            ]
        )
    )
    mean_one, scale_one = statistics(totals[0], totals[1], members, per)
    mean_two, scale_two = statistics(totals[2], totals[3], members, per)
    centred_one = (field_one - mean_one) * scale_one
    scaled_one = centred_one * gains[0]
    active_one = (scaled_one * jax.nn.sigmoid(scaled_one)).astype(jnp.bfloat16)
    centred_two = (field_two - mean_two) * scale_two
    scaled_two = centred_two * gains[1]
    active_two = (scaled_two * jax.nn.sigmoid(scaled_two)).astype(jnp.bfloat16)
    upstream_two = own(cotangent)
    term_two, back_two = layer_back(active_two, upstream_two, kernel_two, half)
    grad_two, weighted_two = norm_back(
        back_two, own(centred_two), own(scaled_two), own(gains[1]), own(scale_two), members, per
    )
    grad_hidden = grad_two.astype(jnp.bfloat16)
    term_one, back_one = layer_back(active_one, grad_hidden, kernel_one, half)
    start = jnp.int32(0)
    combined = lax.psum_scatter(
        jnp.stack(
            [
                term_one(start, lax.axis_size(("tm", "space")) * share),
                term_two(start, lax.axis_size(("tm", "space")) * share),
            ],
            axis=1,
        ),
        ("tm", "space"),
        scatter_dimension=0,
        tiled=True,
    )
    delta_one = combined[:, 0]
    delta_two = combined[:, 1]
    grad_one, weighted_one = norm_back(
        back_one, own(centred_one), own(scaled_one), own(gains[0]), own(scale_one), members, per
    )
    feature_grad = (own(cotangent).astype(jnp.float32) + grad_one).astype(jnp.bfloat16)
    return (feature_grad, delta_one, delta_two, jnp.stack([weighted_one, weighted_two]))


def solution(mesh):
    placed = (
        P(("clip", "tm"), "space", None, None),
        P(("clip", "tm"), "space", None, None),
        P(("clip", "tm"), "space", None, None),
        P(None, None, None, None, "chan"),
        P(None, None, None, None, "chan"),
        P(),
    )
    return jax.shard_map(
        shards,
        mesh=mesh,
        in_specs=placed,
        out_specs=(
            P(("clip", "tm"), "space", None, "chan"),
            P(("clip", "tm", "space"), None, None, None, "chan"),
            P(("clip", "tm", "space"), None, None, None, "chan"),
            P("clip", "chan"),
        ),
        check_vma=False,
    )
```

profile of v0, /device:TPU:0, one launch (start us, length us, event | category | flops | bytes accessed | tf_op | source)
XLA Modules:
  0.0 289.6 jit_solution(4879320679843734137)
XLA Ops:
  7.2 1.1 constant_dynamic-slice_fusion.2
  8.4 4.9 %collective-permute-start = (bf16[2,1,90,128]{3,2,1,0:T(8,128)(2,1)S(1)}, bf16[2,1,90,128]{3,2,1,0:T(8,128)(2,1)S(1)}, u32[]{:S(2)}, u32[]{:S(2)}) collective-permute-start(bf16[2,1,90,128]{3,2,1,0:T(8,128)(2,1)S(1)} %get-tuple-element.41), channel_id=1, source_target_pairs={{0,2},{1,3},{4,6},{5,7},{8,10},{9,11},{12,14},{13,15},{16,18},{17,... | collective-permute-start | bytes 138248 | tf_op jit(solution)/shard_map/ppermute | solution.py:20
  13.3 1.3 collective-permute-start.1
  14.6 0.4 collective-permute-done
  15.1 4.2 %collective-permute-done.1 = bf16[2,1,90,128]{3,2,1,0:T(8,128)(2,1)S(1)} collective-permute-done((bf16[2,1,90,128]{3,2,1,0:T(8,128)(2,1)S(1)}, bf16[2,1,90,128]{3,2,1,0:T(8,128)(2,1)S(1)}, u32[]{:S(2)}, u32[]{:S(2)}) %collective-permute-start.1) | collective-permute-done | bytes 46112 | tf_op jit(solution)/shard_map/ppermute | solution.py:22
  19.3 1.3 collective-permute-start.2
  20.6 7.9 %collective-permute-done.2 = bf16[2,6,90,128]{3,2,1,0:T(8,128)(2,1)S(1)} collective-permute-done((bf16[2,6,90,128]{3,2,1,0:T(8,128)(2,1)S(1)}, bf16[2,6,90,128]{3,2,1,0:T(8,128)(2,1)S(1)}, u32[]{:S(2)}, u32[]{:S(2)}) %collective-permute-start.2) | collective-permute-done | bytes 276512 | tf_op jit(solution)/shard_map/ppermute | solution.py:32
  30.3 2.3 copy-done.3
  32.7 2.5 convolution_bitcast_fusion.2
  35.2 0.2 convert_reduce_fusion.1
  35.4 0.2 convert_reduce_fusion
  35.6 18.1 %psum.21 = f32[4,256]{1,0:T(4,128)S(1)} all-reduce(f32[4,256]{1,0:T(4,128)S(1)} %pad_maximum_fusion.8), channel_id=1, replica_groups=mesh['clip'=2,'tm'=4,'space'=2,'chan'=2] {'tm','space'}, use_global_device_ids=true, to_apply=%region_4.0 | all-reduce | flops 1024 | bytes 8192 | tf_op jit(solution)/shard_map/psum | solution.py:36
  53.9 0.1 reduce_sum.151
  54.6 1.0 multiply_convert_fusion
  55.6 1.2 fusion.37
  56.8 18.2 %psum.22 = f32[2,128]{1,0:T(2,128)S(1)} all-reduce(f32[2,128]{1,0:T(2,128)S(1)} %pad_maximum_fusion.9), channel_id=1, replica_groups=mesh['clip'=2,'tm'=4,'space'=2,'chan'=2] {'tm','space'}, use_global_device_ids=true, to_apply=%region_12.13 | all-reduce | flops 256 | bytes 2048 | tf_op jit(solution)/shard_map/psum | solution.py:36
  75.5 0.1 reduce_sum.155
  75.9 2.9 collective-permute-start.3
  78.8 1.3 collective-permute-start.4
  80.1 0.4 collective-permute-done.3
  80.5 4.3 %collective-permute-done.4 = bf16[2,1,90,128]{3,2,1,0:T(8,128)(2,1)S(1)} collective-permute-done((bf16[2,1,90,128]{3,2,1,0:T(8,128)(2,1)S(1)}, bf16[2,1,90,128]{3,2,1,0:T(8,128)(2,1)S(1)}, u32[]{:S(2)}, u32[]{:S(2)}) %collective-permute-start.4) | collective-permute-done | bytes 46112 | tf_op jit(solution)/shard_map/ppermute | solution.py:22
  84.8 1.3 collective-permute-start.5
  86.2 0.1 reduce_sum.149
  86.4 0.1 reduce_sum.148
  86.9 6.5 %collective-permute-done.5 = bf16[2,6,90,128]{3,2,1,0:T(8,128)(2,1)S(1)} collective-permute-done((bf16[2,6,90,128]{3,2,1,0:T(8,128)(2,1)S(1)}, bf16[2,6,90,128]{3,2,1,0:T(8,128)(2,1)S(1)}, u32[]{:S(2)}, u32[]{:S(2)}) %collective-permute-start.5) | collective-permute-done | bytes 276512 | tf_op jit(solution)/shard_map/ppermute | solution.py:32
  95.2 0.4 copy-done.10
  95.6 1.6 fusion
  97.3 0.3 copy-done.4
  97.5 1.0 copy.113
  98.5 0.2 reduce-scatter.8.cloned.1.call-start
  98.8 0.3 multiply_convert_fusion.1
  99.3 4.6 %copy.72 = bf16[2,4,90,27,128]{4,3,2,1,0:T(8,128)(2,1)S(1)} copy(bf16[2,4,90,27,128]{4,2,3,1,0:T(8,128)(2,1)} %copy-done.3) | data formatting | bytes 9953280 | tf_op jit(solution)/shard_map/stack | solution.py:76
  103.9 7.3 %copy.111 = bf16[90,8,27,128]{3,1,2,0:T(8,128)(2,1)} copy(bf16[90,8,27,128]{3,2,1,0:T(8,128)(2,1)S(1)} %bitcast.258) | data formatting | bytes 9953280
  111.2 7.9 %copy.73 = bf16[3456,720]{1,0:T(8,128)(2,1)} copy(bf16[3456,720]{0,1:T(8,128)(2,1)} %bitcast.262) | data formatting | bytes 9953280 | tf_op jit(solution)/shard_map/dot_general | solution.py:85
  119.1 6.0 %convolution_bitcast_fusion = f32[256,1,3,3,3,128]{5,0,4,3,2,1:T(8,128)} fusion(bf16[3,3,3,128,720]{4,3,2,1,0:T(8,128)(2,1)} %bitcast.260, bf16[720,256,1,1,1]{1,0,2,3,4:T(8,128)(2,1)S(1)} %reshape.335), kind=kOutput, calls=%fused_computation.5 | convolution fusion | flops 1274019840 | bytes 8884224 | tf_op jit(solution)/shard_map/dot_general | solution.py:85
  125.1 5.8 %copy.69 = bf16[2,4,90,27,128]{4,3,2,1,0:T(8,128)(2,1)S(1)} copy(bf16[2,4,90,27,128]{4,2,1,0,3:T(8,128)(2,1)} %copy-done.4) | data formatting | bytes 9953280 | tf_op jit(solution)/shard_map/stack | solution.py:76
  130.9 7.3 %copy.112 = bf16[90,8,27,128]{3,1,2,0:T(8,128)(2,1)} copy(bf16[90,8,27,128]{3,2,1,0:T(8,128)(2,1)S(1)} %bitcast.259) | data formatting | bytes 9953280
  138.2 8.0 %copy.70 = bf16[3456,720]{1,0:T(8,128)(2,1)} copy(bf16[3456,720]{0,1:T(8,128)(2,1)} %bitcast.263) | data formatting | bytes 9953280 | tf_op jit(solution)/shard_map/dot_general | solution.py:85
  146.2 4.3 %convolution_bitcast_fusion.1 = f32[256,1,3,3,3,128]{5,0,4,3,2,1:T(8,128)S(1)} fusion(bf16[3,3,3,128,720]{4,3,2,1,0:T(8,128)(2,1)} %bitcast.261, bf16[720,256,1,1,1]{1,0,2,3,4:T(8,128)(2,1)S(1)} %reshape.334), kind=kOutput, calls=%fused_computation.6 | convolution fusion | flops 1274019840 | bytes 8884224 | tf_op jit(solution)/shard_map/dot_general | solution.py:85
  150.5 3.4 %pad_maximum_fusion = f32[256,2,3,3,3,128]{5,0,4,3,2,1:T(8,128)} fusion(f32[256,1,3,3,3,128]{5,0,4,3,2,1:T(8,128)S(1)} %copy-done.2, f32[256,1,3,3,3,128]{5,0,4,3,2,1:T(8,128)S(1)} %convolution_bitcast_fusion.1), kind=kLoop, calls=%fused_computation | loop fusion | flops 1769472 | bytes 14155776 | tf_op jit(solution)/shard_map/stack | solution.py:153
  154.0 2.0 fusion.36
  156.0 18.2 %psum.23 = f32[2,128]{1,0:T(2,128)S(1)} all-reduce(f32[2,128]{1,0:T(2,128)S(1)} %pad_maximum_fusion.10), channel_id=1, replica_groups=mesh['clip'=2,'tm'=4,'space'=2,'chan'=2] {'tm','space'}, use_global_device_ids=true, to_apply=%region_18.19 | all-reduce | flops 256 | bytes 2048 | tf_op jit(solution)/shard_map/psum | solution.py:36
  174.7 0.1 reduce_sum.159
  175.0 1.1 add_convert_fusion
  176.1 0.8 copy.75
  176.9 0.6 pad_maximum_fusion.11
  177.5 103.5 %reduce-scatter.8.cloned.1.call-done = f32[32,2,3,3,3,128]{5,0,4,3,2,1:T(8,128)} async-done(((f32[256,2,3,3,3,128]{5,0,4,3,2,1:T(8,128)}), f32[32,2,3,3,3,128]{5,0,4,3,2,1:T(8,128)}) %reduce-scatter.8.cloned.1.call-update) | async-done | bytes 884752 | tf_op jit(solution)/shard_map/reduce_scatter | solution.py:152
  281.0 2.1 slice_bitcast_fusion
  (134 shorter events, 6.7 us)
Async XLA Ops:
  7.2 23.1 %copy-start = (bf16[256,3,3,3,128]{4,0,3,2,1:T(8,128)(2,1)S(1)}, bf16[256,3,3,3,128]{4,0,3,2,1:T(8,128)(2,1)}, u32[]{:S(2)}) copy-start(bf16[256,3,3,3,128]{4,0,3,2,1:T(8,128)(2,1)} %param.10) | copy-start | bytes 5308420
  7.2 48.4 %reduce-scatter.4.cloned.1.call-start = ((), (), s32[]{:S(2)}) async-start(), calls=%async_computation.3 | async-start | bytes 1179648 | tf_op jit(solution)/shard_map/reduce_scatter | solution.py:104
  8.4 6.6 %collective-permute-start = (bf16[2,1,90,128]{3,2,1,0:T(8,128)(2,1)S(1)}, bf16[2,1,90,128]{3,2,1,0:T(8,128)(2,1)S(1)}, u32[]{:S(2)}, u32[]{:S(2)}) collective-permute-start(bf16[2,1,90,128]{3,2,1,0:T(8,128)(2,1)S(1)} %get-tuple-element.41), channel_id=1, source_target_pairs={{0,2},{1,3},{4,6},{5,7},{8,10},{9,11},{12,14},{13,15},{16,18},{17,... | collective-permute-start | bytes 138248 | tf_op jit(solution)/shard_map/ppermute | solution.py:20
  13.3 6.0 %collective-permute-start.1 = (bf16[2,1,90,128]{3,2,1,0:T(8,128)(2,1)S(1)}, bf16[2,1,90,128]{3,2,1,0:T(8,128)(2,1)S(1)}, u32[]{:S(2)}, u32[]{:S(2)}) collective-permute-start(bf16[2,1,90,128]{3,2,1,0:T(8,128)(2,1)S(1)} %get-tuple-element.40), channel_id=1, source_target_pairs={{2,0},{3,1},{6,4},{7,5},{10,8},{11,9},{14,12},{15,13},{18,16},{19,... | collective-permute-start | bytes 138248 | tf_op jit(solution)/shard_map/ppermute | solution.py:22
  19.3 9.2 %collective-permute-start.2 = (bf16[2,6,90,128]{3,2,1,0:T(8,128)(2,1)S(1)}, bf16[2,6,90,128]{3,2,1,0:T(8,128)(2,1)S(1)}, u32[]{:S(2)}, u32[]{:S(2)}) collective-permute-start(bf16[2,6,90,128]{3,2,1,0:T(8,128)(2,1)S(1)} %constant_dynamic-update-slice_fusion), channel_id=1, source_target_pairs={{4,0},{8,4},{12,8},{5,1},{9,5},{13,9},{6,2},{10,6},{14,10},{7,3},{... | collective-permute-start | bytes 829448 | tf_op jit(solution)/shard_map/ppermute | solution.py:32
  30.3 2.3 copy-start.3
  30.3 4.9 %copy-start.7 = (bf16[2,4,90,256]{3,1,2,0:T(4,128)(2,1)S(1)}, bf16[2,4,90,256]{3,1,2,0:T(4,128)(2,1)}, u32[]{:S(2)}) copy-start(bf16[2,4,90,256]{3,1,2,0:T(4,128)(2,1)} %param.6) | copy-start | bytes 1105924
  32.7 2.7 copy-start.6
  32.7 21.9 %copy-start.9 = (f32[2,256]{1,0:T(2,128)S(1)}, f32[2,256]{1,0:T(2,128)}, u32[]{:S(2)}) copy-start(f32[2,256]{1,0:T(2,128)} %param.11) | copy-start | bytes 6148
  35.2 118.8 %reduce-scatter.6.cloned.1.call-start = ((), (), s32[]{:S(2)}) async-start(), calls=%async_computation.4 | async-start | bytes 1179648 | tf_op jit(solution)/shard_map/reduce_scatter | solution.py:104
  75.9 4.6 %collective-permute-start.3 = (bf16[2,1,90,128]{3,2,1,0:T(8,128)(2,1)S(1)}, bf16[2,1,90,128]{3,2,1,0:T(8,128)(2,1)S(1)}, u32[]{:S(2)}, u32[]{:S(2)}) collective-permute-start(bf16[2,1,90,128]{3,2,1,0:T(8,128)(2,1)S(1)} %get-tuple-element.38), channel_id=1, source_target_pairs={{0,2},{1,3},{4,6},{5,7},{8,10},{9,11},{12,14},{13,15},{16,18},{17,... | collective-permute-start | bytes 138248 | tf_op jit(solution)/shard_map/ppermute | solution.py:20
  78.8 6.0 %collective-permute-start.4 = (bf16[2,1,90,128]{3,2,1,0:T(8,128)(2,1)S(1)}, bf16[2,1,90,128]{3,2,1,0:T(8,128)(2,1)S(1)}, u32[]{:S(2)}, u32[]{:S(2)}) collective-permute-start(bf16[2,1,90,128]{3,2,1,0:T(8,128)(2,1)S(1)} %get-tuple-element.39), channel_id=1, source_target_pairs={{2,0},{3,1},{6,4},{7,5},{10,8},{11,9},{14,12},{15,13},{18,16},{19,... | collective-permute-start | bytes 138248 | tf_op jit(solution)/shard_map/ppermute | solution.py:22
  84.8 8.6 %collective-permute-start.5 = (bf16[2,6,90,128]{3,2,1,0:T(8,128)(2,1)S(1)}, bf16[2,6,90,128]{3,2,1,0:T(8,128)(2,1)S(1)}, u32[]{:S(2)}, u32[]{:S(2)}) collective-permute-start(bf16[2,6,90,128]{3,2,1,0:T(8,128)(2,1)S(1)} %pad_maximum_fusion.3), channel_id=1, source_target_pairs={{4,0},{8,4},{12,8},{5,1},{9,5},{13,9},{6,2},{10,6},{14,10},{7,3},{... | collective-permute-start | bytes 829448 | tf_op jit(solution)/shard_map/ppermute | solution.py:32
  94.2 1.5 copy-start.10
  95.2 2.3 copy-start.4
  95.6 3.1 %copy-start.8 = (bf16[2,4,90,256]{3,1,2,0:T(4,128)(2,1)S(1)}, bf16[2,4,90,256]{3,1,2,0:T(4,128)(2,1)}, u32[]{:S(2)}) copy-start(bf16[2,4,90,256]{3,1,2,0:T(4,128)(2,1)} %param.6) | copy-start | bytes 1105924
  97.5 1.6 copy-start.5
  98.5 182.5 %reduce-scatter.8.cloned.1.call-start = ((), (), s32[]{:S(2)}) async-start(), calls=%async_computation.5 | async-start | bytes 7962624 | tf_op jit(solution)/shard_map/reduce_scatter | solution.py:152
  146.2 4.3 %copy-start.2 = (f32[256,1,3,3,3,128]{5,0,4,3,2,1:T(8,128)S(1)}, f32[256,1,3,3,3,128]{5,0,4,3,2,1:T(8,128)}, u32[]{:S(2)}) copy-start(f32[256,1,3,3,3,128]{5,0,4,3,2,1:T(8,128)} %convolution_bitcast_fusion) | copy-start | bytes 10616836
  153.9 129.2 %copy-start.1 = (bf16[256,3,3,3,128]{4,0,3,2,1:T(8,128)(2,1)S(1)}, bf16[256,3,3,3,128]{4,0,3,2,1:T(8,128)(2,1)}, u32[]{:S(2)}) copy-start(bf16[256,3,3,3,128]{4,0,3,2,1:T(8,128)(2,1)} %param.10) | copy-start | bytes 5308420
Sparse Core Ops, SparseCore 0:
  35.3 7.4 reduce-scatter.3
  98.6 5.4 reduce-scatter.5
  154.0 126.9 reduce-scatter.7
where the time goes:
time: 291 us; the launch traced here: 290 us
  waiting for transfers between devices  127 us (44%)
  blocking collectives  54.5 us (19%)
  local copies, waits for them, and re-layouts  54.4 us (19%)
  matrix products  14.5 us (5%)
  between operations  14.3 us (5%)
  starting transfers between devices  13.2 us (5%)
  other arithmetic  11.5 us (4%)
    reduce_scatter x1, waiting for transfers between devices, shards(): lax.psum_scatter(jnp.stack([term_one(start, lax.axis_size(('tm', 'space')...  104 us
    psum x3, blocking collectives, clip_totals(): return lax.psum(values, ('tm', 'space'))  54.5 us
    unnamed x73, local copies, waits for them, and re-layouts  21.3 us
    dot_general x2, local copies, waits for them, and re-layouts, term(): lax.dot_general(flat_active, flat_taps, (((0,), (0,)), ((), ())), preferr...  15.9 us
    ppermute x2, waiting for transfers between devices, passed_along(): return lax.ppermute(block, axis, route)  14.5 us
    another operation x4, local copies, waits for them, and re-layouts, tap_stack(): stacked = jnp.stack(pieces, axis=3)  10.6 us
    dot_general x2, matrix products, term(): lax.dot_general(flat_active, flat_taps, (((0,), (0,)), ((), ())), preferr...  10.3 us
    ppermute x2, waiting for transfers between devices, extended_2(): lax.ppermute(head, axis, [((i + 1) % count, i) for i in range(ends)])  8.45 us
  transfers between devices with their start and end apart: 9, of which 7 were waited for; matrix products, arithmetic and copies ran while one was open for 22% of the time, Pallas kernels for 0%

commit v1 on v0

v1 whole, which is shorter than its diff:
```python
import jax
import jax.numpy as jnp
from jax import lax
from jax.experimental import pallas as pl
from jax.experimental.pallas import tpu as pltpu
from jax.sharding import PartitionSpec as P

GROUPS = 32


epsilon = 1e-06


CLIP = ("tm", "space")


def clip_totals(values):
    count = lax.axis_size(CLIP)
    if count & (count - 1):
        return lax.psum(values, CLIP)
    step = 1
    while step < count:
        values = values + lax.ppermute(values, CLIP, [(i, i ^ step) for i in range(count)])
        step *= 2
    return values


def statistics(total, square, members, per):
    mean = jnp.sum(total.reshape(-1, per), axis=1) / members
    spread = jnp.sum(square.reshape(-1, per), axis=1) / members - mean * mean
    scale = lax.rsqrt(spread + epsilon)
    return (jnp.repeat(mean, per), jnp.repeat(scale, per))


def norm_back(upstream, centred, scaled, gain, scale, members, per):
    gate = jax.nn.sigmoid(scaled)
    slope = upstream * gate * (1.0 + scaled * (1.0 - gate))
    totals = clip_totals(
        jnp.stack([jnp.sum(slope, axis=(0, 1, 2)), jnp.sum(slope * centred, axis=(0, 1, 2))])
    )
    first = jnp.repeat(jnp.sum((gain * totals[0]).reshape(-1, per), axis=1), per) / members
    second = jnp.repeat(jnp.sum((gain * totals[1]).reshape(-1, per), axis=1), per) / members
    return (scale * (slope * gain - first - centred * second), totals[1])


def tap_stack(extended, frames, height, width):
    pieces = []
    for frame_tap in range(3):
        for row_tap in range(3):
            for col_tap in range(3):
                pieces.append(
                    extended[
                        2 - frame_tap : 2 - frame_tap + frames,
                        2 - row_tap : 2 - row_tap + height,
                        2 - col_tap : 2 - col_tap + width,
                    ]
                )
    stacked = jnp.stack(pieces, axis=3)
    return stacked.reshape(frames * height * width, 27, extended.shape[3])


def rounded_up(size, unit):
    return -(-size // unit) * unit


def gathered(grad, wide):
    rows = lax.all_gather(grad, "space", axis=1, tiled=True)
    whole = lax.all_gather(rows, "tm", axis=0, tiled=True)
    return jnp.pad(whole, ((0, 2), (1, 1), (0, wide - grad.shape[2]), (0, 0)))


def channel_shares(field, wide, share, rows):
    frames, height, width, channels = field.shape
    count = channels // share
    field = jnp.pad(field, ((0, 0), (0, 0), (0, wide - width), (0, 0)))
    field = field.reshape(frames, height * wide, channels).transpose(0, 2, 1)
    field = field.reshape(frames, count, share, height * wide).transpose(1, 0, 2, 3)
    return jnp.pad(field, ((0, 0), (0, 0), (0, rows - share), (0, 0)))


def exchanged(fields):
    blocks = lax.all_to_all(fields, CLIP, 0, 0, tiled=True)
    tm, space = lax.axis_size("tm"), lax.axis_size("space")
    _, frames, rows, lanes = blocks.shape
    blocks = blocks.reshape(tm, space, frames, rows, lanes).transpose(0, 2, 3, 1, 4)
    return blocks.reshape(tm * frames, rows, space * lanes)


def delta_share(field, mean, scale, gain, padded, width, wide):
    total, rows, lanes = field.shape
    depth = padded.shape[3]
    padded = padded.reshape(padded.shape[0], -1, depth)
    columns = jnp.stack([mean, scale, gain], axis=1)

    def body(field_ref, columns_ref, padded_ref, out_ref):
        frame = pl.program_id(0)

        @pl.when(frame == 0)
        def _():
            out_ref[...] = jnp.zeros_like(out_ref)

        column = columns_ref[...]
        scaled = (field_ref[0].astype(jnp.float32) - column[:, 0:1]) * column[:, 1:2] * column[:, 2:3]
        active = (scaled * jax.nn.sigmoid(scaled)).astype(jnp.bfloat16).astype(jnp.float32)
        place = lax.broadcasted_iota(jnp.int32, active.shape, 1)
        active = jnp.where(place % wide < width, active, 0.0)
        left = jnp.concatenate(
            [pltpu.roll(active, 1, 1), active, pltpu.roll(active, lanes - 1, 1)], axis=0
        ).astype(jnp.bfloat16)
        right = jnp.concatenate(
            [
                padded_ref[frame + 2 - a, (2 - b) * wide : (2 - b) * wide + lanes, :]
                for a in range(3)
                for b in range(3)
            ],
            axis=1,
        )
        out_ref[...] += lax.dot_general(
            left, right, (((1,), (0,)), ((), ())), preferred_element_type=jnp.float32
        )

    out = pl.pallas_call(
        body,
        grid=(total,),
        in_specs=[
            pl.BlockSpec((1, rows, lanes), lambda t: (t, 0, 0)),
            pl.BlockSpec((rows, 3), lambda t: (0, 0)),
            pl.BlockSpec(padded.shape, lambda t: (0, 0, 0)),
        ],
        out_specs=pl.BlockSpec((3 * rows, 9 * depth), lambda t: (0, 0)),
        out_shape=jax.ShapeDtypeStruct((3 * rows, 9 * depth), jnp.float32),
        cost_estimate=pl.CostEstimate(
            flops=2 * total * lanes * 27 * rows * depth, bytes_accessed=4 << 20, transcendentals=0
        ),
        name="delta_share",
    )(field, columns, padded)
    return out.reshape(3, rows, 3, 3, depth).transpose(1, 2, 3, 0, 4)


def summed_over_chan(partial, half):
    if lax.axis_size("chan") != 2:
        return lax.psum_scatter(partial, "chan", scatter_dimension=3, tiled=True)
    own = lax.axis_index("chan") * half
    other = lax.ppermute(
        lax.dynamic_slice_in_dim(partial, half - own, half, 3), "chan", [(0, 1), (1, 0)]
    )
    return lax.dynamic_slice_in_dim(partial, own, half, 3) + other


def gradient_back(padded, kernel, shape):
    frames, height, width, channels = shape
    half = kernel.shape[4]
    start = (lax.axis_index("tm") * frames, lax.axis_index("space") * height, 0, 0)
    near = lax.dynamic_slice(padded, start, (frames + 2, height + 2, width, half))
    near = jnp.pad(near, ((0, 0), (0, 0), (1, 1), (0, 0)))
    taps = tap_stack(near, frames, height, width)
    partial = lax.dot_general(
        taps,
        kernel.reshape(channels, 27, half),
        (((1, 2), (1, 2)), ((), ())),
        preferred_element_type=jnp.float32,
    )
    return summed_over_chan(partial.reshape(frames, height, width, channels), half)


def shards(features, hidden, cotangent, kernel_one, kernel_two, gains):
    frames, height, width, channels = features.shape
    half = kernel_one.shape[4]
    per = channels // GROUPS
    offset = lax.axis_index("chan") * half
    members = float(frames * height * width * per * lax.axis_size(CLIP))
    share = channels // lax.axis_size(CLIP)
    rows = rounded_up(share, 8)
    wide = rounded_up(width, 32)

    def own(field):
        return lax.dynamic_slice_in_dim(field, offset, half, field.ndim - 1)

    def shared(values):
        values = lax.dynamic_slice_in_dim(values, lax.axis_index(CLIP) * share, share, 0)
        return jnp.pad(values, (0, rows - share))

    cotangent_own = own(cotangent)
    padded_two = gathered(cotangent_own, wide)
    field_one = features.astype(jnp.float32)
    field_two = hidden.astype(jnp.float32)
    totals = clip_totals(
        jnp.stack(
            [
                jnp.sum(field_one, axis=(0, 1, 2)),
                jnp.sum(field_one * field_one, axis=(0, 1, 2)),
                jnp.sum(field_two, axis=(0, 1, 2)),
                jnp.sum(field_two * field_two, axis=(0, 1, 2)),
            ]
        )
    )
    both = jnp.concatenate(
        [channel_shares(features, wide, share, rows), channel_shares(hidden, wide, share, rows)],
        axis=2,
    )
    both = exchanged(both)
    mean_one, scale_one = statistics(totals[0], totals[1], members, per)
    mean_two, scale_two = statistics(totals[2], totals[3], members, per)
    centred_one = (own(field_one) - own(mean_one)) * own(scale_one)
    scaled_one = centred_one * own(gains[0])
    centred_two = (own(field_two) - own(mean_two)) * own(scale_two)
    scaled_two = centred_two * own(gains[1])
    back_two = gradient_back(padded_two, kernel_two, features.shape)
    grad_two, weighted_two = norm_back(
        back_two, centred_two, scaled_two, own(gains[1]), own(scale_two), members, per
    )
    delta_two = delta_share(
        both[:, rows:], shared(mean_two), shared(scale_two), shared(gains[1]), padded_two, width, wide
    )
    padded_one = gathered(grad_two.astype(jnp.bfloat16), wide)
    back_one = gradient_back(padded_one, kernel_one, features.shape)
    delta_one = delta_share(
        both[:, :rows], shared(mean_one), shared(scale_one), shared(gains[0]), padded_one, width, wide
    )
    grad_one, weighted_one = norm_back(
        back_one, centred_one, scaled_one, own(gains[0]), own(scale_one), members, per
    )
    feature_grad = (cotangent_own.astype(jnp.float32) + grad_one).astype(jnp.bfloat16)
    return (
        feature_grad,
        delta_one[:share],
        delta_two[:share],
        jnp.stack([weighted_one, weighted_two]),
    )


def solution(mesh):
    placed = (
        P(("clip", "tm"), "space", None, None),
        P(("clip", "tm"), "space", None, None),
        P(("clip", "tm"), "space", None, None),
        P(None, None, None, None, "chan"),
        P(None, None, None, None, "chan"),
        P(),
    )
    return jax.shard_map(
        shards,
        mesh=mesh,
        in_specs=placed,
        out_specs=(
            P(("clip", "tm"), "space", None, "chan"),
            P(("clip", "tm", "space"), None, None, None, "chan"),
            P(("clip", "tm", "space"), None, None, None, "chan"),
            P("clip", "chan"),
        ),
        check_vma=False,
    )
```

time: 291 us -> 212 us (0.73)
  waiting for transfers between devices: 127 us -> 66.5 us
  blocking collectives: 54.5 us -> 14.9 us
  Pallas kernels: 0 us -> 15.8 us
  matrix products: 14.5 us -> 3.23 us
  other arithmetic: 11.5 us -> 22.6 us
  starting transfers between devices: 13.2 us -> 17.6 us
    reduce_scatter x3 -> x0, waiting for transfers between devices: 104 us -> none  [the longest x1 104 us: shards(): lax.psum_scatter(jnp.stack([term_one(start, lax.axis_size(('tm', 'space')...]
    all_gather x0 -> x2, waiting for transfers between devices: none -> 57 us  [gathered(): whole = lax.all_gather(rows, 'tm', axis=0, tiled=True)]
    psum x3 -> x0, blocking collectives: 54.5 us -> none  [clip_totals(): return lax.psum(values, ('tm', 'space'))]
    dot_general x3 -> x0, local copies, waits for them, and re-layouts: 16.8 us -> none  [the longest x2 15.9 us: term(): lax.dot_general(flat_active, flat_taps, (((0,), (0,)), ((), ())), preferr...]
    pallas_call x0 -> x2, Pallas kernels: none -> 15.8 us  [delta_share(): pl.pallas_call(body, grid=(total,), in_specs=[pl.BlockSpec((1, rows, lane...]
    all_gather x0 -> x2, blocking collectives: none -> 14.9 us  [gathered(): rows = lax.all_gather(grad, 'space', axis=1, tiled=True)]
    ppermute x6 -> x11, waiting for transfers between devices: 23.8 us -> 9.49 us  [the longest x9 9.48 us: clip_totals(): lax.ppermute(values, CLIP, [(i, i ^ step) for i in range(count)])]
    unnamed x73 -> x84, local copies, waits for them, and re-layouts: 21.3 us -> 10.1 us
  transfers between devices with their start and end apart: 9 -> 14, of which waited for: 7 -> 6; matrix products, arithmetic and copies ran while one was open for 22% -> 30% of each run, Pallas kernels for 0% -> 7%
where the time goes in v1:
time: 212 us; the launch traced here: 210 us
  waiting for transfers between devices  66.5 us (31%)
  local copies, waits for them, and re-layouts  55.2 us (26%)
  other arithmetic  22.6 us (11%)
  starting transfers between devices  17.6 us (8%)
  Pallas kernels  15.8 us (7%)
  blocking collectives  14.9 us (7%)
  between operations  14.5 us (7%)
  matrix products  3.23 us (2%)
    all_gather x2, waiting for transfers between devices, gathered(): whole = lax.all_gather(rows, 'tm', axis=0, tiled=True)  57 us
    pallas_call x2, Pallas kernels, delta_share(): pl.pallas_call(body, grid=(total,), in_specs=[pl.BlockSpec((1, rows, lane...  15.8 us
    all_gather x2, blocking collectives, gathered(): rows = lax.all_gather(grad, 'space', axis=1, tiled=True)  14.9 us
    ppermute x9, starting transfers between devices, clip_totals(): lax.ppermute(values, CLIP, [(i, i ^ step) for i in range(count)])  13.2 us
    unnamed x84, local copies, waits for them, and re-layouts  10.1 us
    ppermute x9, waiting for transfers between devices, clip_totals(): lax.ppermute(values, CLIP, [(i, i ^ step) for i in range(count)])  9.48 us
    reduce_sum x2, other arithmetic, norm_back(): jnp.sum(slope, axis=(0, 1, 2))  4.41 us
    all_to_all x1, starting transfers between devices, exchanged(): blocks = lax.all_to_all(fields, CLIP, 0, 0, tiled=True)  4.39 us
  transfers between devices with their start and end apart: 14, of which 6 were waited for; matrix products, arithmetic and copies ran while one was open for 30% of the time, Pallas kernels for 7%

profile of v1, /device:TPU:0, one launch (start us, length us, event | category | flops | bytes accessed | tf_op | source)
XLA Modules:
  0.0 210.3 jit_solution(11154444140256211105)
XLA Ops:
  7.2 1.1 constant_dynamic-slice_fusion.7
  8.4 8.5 %all_gather.12 = bf16[2,8,90,128]{3,2,1,0:T(8,128)(2,1)S(1)} all-gather(bf16[2,4,90,128]{3,2,1,0:T(8,128)(2,1)S(1)} %copy.144), channel_id=1, replica_groups=mesh['clip'=2,'tm'=4,'space'=2,'chan'=2] {'space'}, dimensions={1}, use_global_device_ids=true | all-gather | bytes 552960 | tf_op jit(solution)/shard_map/all_gather | solution.py:67
  17.9 1.1 convert_reduce_fusion.1
  19.0 1.1 convert_reduce_fusion
  20.2 1.8 collective-permute-start
  22.0 2.1 fusion.14
  24.1 1.7 collective-permute-start.1
  26.5 1.2 collective-permute-done.1
  27.8 2.7 %collective-permute-start.2 = (f32[4,256]{1,0:T(4,128)S(1)}, f32[4,256]{1,0:T(4,128)S(1)}, u32[]{:S(2)}, u32[]{:S(2)}) collective-permute-start(f32[4,256]{1,0:T(4,128)S(1)} %fusion.22), channel_id=1, source_target_pairs={{0,8},{2,10},{4,12},{6,14},{8,0},{10,2},{12,4},{14,6},{1,9},{3,11}... | collective-permute-start | bytes 12296 | tf_op jit(solution)/shard_map/ppermute | solution.py:23
  30.5 24.5 %all-gather.3.cloned.1.call-done = bf16[8,8,90,128]{3,1,2,0:T(8,128)(2,1)} async-done(((bf16[2,8,90,128]{3,1,2,0:T(8,128)(2,1)}), bf16[8,8,90,128]{3,1,2,0:T(8,128)(2,1)}) %all-gather.3.cloned.1.call-update) | async-done | bytes 1474576 | tf_op jit(solution)/shard_map/all_gather | solution.py:68
  54.9 1.7 copy.98
  58.9 1.6 convolution_bitcast_fusion.1
  64.1 1.4 reshape_squeeze.15
  67.0 1.2 broadcast_multiply_fusion.4
  68.9 1.3 dynamic_slice.69
  72.4 2.2 %fusion.10 = (f32[128]{0:T(128)S(1)}, f32[128]{0:T(128)S(1)}, f32[2,4,90,128]{3,2,1,0:T(8,128)}) fusion(f32[128]{0:T(128)} %dynamic_slice.69, f32[128]{0:T(128)S(1)} %dynamic_slice.74, f32[2,4,90,256]{3,2,1,0:T(8,128)} %get-tuple-element.41, s32[]{:T(128)S(6)} %select_n.10, f32[128]{0:T(128)} %fusion.4, f32[2,4,90,128]{3,2,1,0:T(8,128)} %collective-permute-done.3, ...), kind=kLoop, calls=%fused_computation.135 | loop fusion | flops 1382144 | bytes 1477124 | tf_op jit(solution)/shard_map/reduce_sum | solution.py:39
  74.6 1.5 collective-permute-start.4
  76.1 2.1 %collective-permute-done.4 = f32[2,128]{1,0:T(2,128)S(1)} collective-permute-done((f32[2,128]{1,0:T(2,128)S(1)}, f32[2,128]{1,0:T(2,128)S(1)}, u32[]{:S(2)}, u32[]{:S(2)}) %collective-permute-start.4) | collective-permute-done | bytes 1056 | tf_op jit(solution)/shard_map/ppermute | solution.py:23
  79.0 2.9 %collective-permute-done.5 = f32[2,128]{1,0:T(2,128)S(1)} collective-permute-done((f32[2,128]{1,0:T(2,128)S(1)}, f32[2,128]{1,0:T(2,128)S(1)}, u32[]{:S(2)}, u32[]{:S(2)}) %collective-permute-start.5) | collective-permute-done | bytes 1056 | tf_op jit(solution)/shard_map/ppermute | solution.py:23
  81.9 1.4 collective-permute-start.6
  83.2 3.2 %collective-permute-done.6 = f32[2,128]{1,0:T(2,128)S(1)} collective-permute-done((f32[2,128]{1,0:T(2,128)S(1)}, f32[2,128]{1,0:T(2,128)S(1)}, u32[]{:S(2)}, u32[]{:S(2)}) %collective-permute-start.6) | collective-permute-done | bytes 1056 | tf_op jit(solution)/shard_map/ppermute | solution.py:23
  86.4 1.1 multiply_reduce_fusion.7
  90.6 1.2 multiply_convert_fusion
  91.9 6.3 %all_gather.14 = bf16[2,8,90,128]{3,2,1,0:T(8,128)(2,1)S(1)} all-gather(bf16[2,4,90,128]{3,2,1,0:T(8,128)(2,1)S(1)} %multiply_convert_fusion), channel_id=1, replica_groups=mesh['clip'=2,'tm'=4,'space'=2,'chan'=2] {'space'}, dimensions={1}, use_global_device_ids=true | all-gather | bytes 552960 | tf_op jit(solution)/shard_map/all_gather | solution.py:67
  99.1 2.0 fusion.13
  101.9 1.9 copy.130
  103.8 1.8 pad.26
  105.6 1.9 copy.132
  107.5 1.2 pad_maximum_fusion
  108.7 1.0 copy.133
  109.7 4.4 %all-to-all-start = ((bf16[8,2,64,384]{3,2,1,0:T(8,128)(2,1)}), bf16[8,2,64,384]{3,2,1,0:T(8,128)(2,1)}, u32[]{:S(2)}, u32[]{:S(2)}) async-start(bf16[8,2,64,384]{3,2,1,0:T(8,128)(2,1)} %copy.133), calls=%async_computation | async-start | bytes 1572864 | tf_op jit(solution)/shard_map/all_to_all | solution.py:82
  117.8 32.5 %all-gather.5.cloned.1.call-done = bf16[8,8,90,128]{3,1,2,0:T(8,128)(2,1)} async-done(((bf16[2,8,90,128]{3,1,2,0:T(8,128)(2,1)}), bf16[8,8,90,128]{3,1,2,0:T(8,128)(2,1)}) %all-gather.5.cloned.1.call-update) | async-done | bytes 1474576 | tf_op jit(solution)/shard_map/all_gather | solution.py:68
  150.3 1.6 copy.126
  154.9 1.6 convolution_bitcast_fusion
  161.0 2.8 %copy.134 = bf16[4,2,64,2,384]{4,3,2,1,0:T(2,128)(2,1)} copy(bf16[4,2,64,2,384]{4,2,1,3,0:T(8,128)(2,1)} %bitcast.108) | data formatting | bytes 1572864 | tf_op jit(solution)/shard_map/transpose | solution.py:85
  163.8 3.1 %reshape.351 = bf16[8,64,768]{2,1,0:T(8,128)(2,1)} reshape(bf16[4,2,64,2,384]{4,3,2,1,0:T(2,128)(2,1)} %copy.134) | data formatting | bytes 1572864 | tf_op jit(solution)/shard_map/reshape | solution.py:86
  166.9 2.2 %fusion.9 = (f32[128]{0:T(128)S(1)}, f32[128]{0:T(128)S(1)}, f32[2,4,90,128]{3,2,1,0:T(8,128)}) fusion(f32[128]{0:T(128)S(1)} %dynamic_slice.68, f32[128]{0:T(128)} %dynamic_slice.80, f32[2,4,90,256]{3,2,1,0:T(8,128)} %get-tuple-element.39, s32[]{:T(128)S(6)} %select_n.10, f32[128]{0:T(128)S(1)} %copy-done.7, f32[2,4,90,128]{3,2,1,0:T(8,128)} %collective-permute-done.7, ...), kind=kLoop, calls=%fused_computation.134 | loop fusion | flops 1382144 | bytes 1477124 | tf_op jit(solution)/shard_map/reduce_sum | solution.py:39
  169.2 1.6 collective-permute-start.8
  170.8 2.1 fusion.12
  172.9 1.8 pad.21
  174.8 7.9 %delta_share.3 = f32[96,1152]{1,0:T(8,128)} custom-call(bf16[8,32,768]{2,1,0:T(8,128)(2,1)} %get-tuple-element.34.field_ref, f32[32,3]{1,0:T(8,128)} %copy.137.columns_ref, bf16[10,960,128]{2,1,0:T(8,128)(2,1)} %bitcast.224), custom_call_target="tpu_custom_call" | custom-call | flops 1358954496 | bytes 4194304 | tf_op jit(solution)/shard_map/delta_share/pallas_call | solution.py:122
  182.7 2.0 reshape.355
  184.7 1.9 copy.140
  186.7 1.8 pad.23.clone
  188.6 1.7 collective-permute-start.10
  190.3 7.8 %delta_share.2 = f32[96,1152]{1,0:T(8,128)} custom-call(bf16[8,32,768]{2,1,0:T(8,128)(2,1)} %get-tuple-element.35.field_ref, f32[32,3]{1,0:T(8,128)} %copy.136.columns_ref, bf16[10,960,128]{2,1,0:T(8,128)(2,1)} %bitcast.223), custom_call_target="tpu_custom_call" | custom-call | flops 1358954496 | bytes 4194304 | tf_op jit(solution)/shard_map/delta_share/pallas_call | solution.py:122
  198.1 1.2 reshape.353
  201.0 1.1 add_convert_fusion
  (172 shorter events, 31.6 us)
Async XLA Ops:
  7.2 51.8 %copy-start = (bf16[256,3,3,3,128]{4,0,3,2,1:T(8,128)(2,1)S(1)}, bf16[256,3,3,3,128]{4,0,3,2,1:T(8,128)(2,1)}, u32[]{:S(2)}) copy-start(bf16[256,3,3,3,128]{4,0,3,2,1:T(8,128)(2,1)} %param.10) | copy-start | bytes 5308420
  7.2 47.8 %all-gather.3.cloned.1.call-start = ((), (), s32[]{:S(2)}) async-start(), calls=%async_computation.1 | async-start | bytes 1843200 | tf_op jit(solution)/shard_map/all_gather | solution.py:68
  17.8 132.5 %all-gather.5.cloned.1.call-start = ((), (), s32[]{:S(2)}) async-start(), calls=%async_computation.2 | async-start | bytes 1843200 | tf_op jit(solution)/shard_map/all_gather | solution.py:68
  20.2 3.9 %collective-permute-start = (f32[4,256]{1,0:T(4,128)S(1)}, f32[4,256]{1,0:T(4,128)S(1)}, u32[]{:S(2)}, u32[]{:S(2)}) collective-permute-start(f32[4,256]{1,0:T(4,128)S(1)} %pad_maximum_fusion.1), channel_id=1, source_target_pairs={{0,2},{2,0},{4,6},{6,4},{8,10},{10,8},{12,14},{14,12},{1,3},{3,1},... | collective-permute-start | bytes 12296 | tf_op jit(solution)/shard_map/ppermute | solution.py:23
  24.1 3.7 %collective-permute-start.1 = (f32[4,256]{1,0:T(4,128)S(1)}, f32[4,256]{1,0:T(4,128)S(1)}, u32[]{:S(2)}, u32[]{:S(2)}) collective-permute-start(f32[4,256]{1,0:T(4,128)S(1)} %fusion.8), channel_id=1, source_target_pairs={{0,4},{2,6},{4,0},{6,2},{8,12},{10,14},{12,8},{14,10},{1,5},{3,7},... | collective-permute-start | bytes 12296 | tf_op jit(solution)/shard_map/ppermute | solution.py:23
  27.8 34.9 %collective-permute-start.2 = (f32[4,256]{1,0:T(4,128)S(1)}, f32[4,256]{1,0:T(4,128)S(1)}, u32[]{:S(2)}, u32[]{:S(2)}) collective-permute-start(f32[4,256]{1,0:T(4,128)S(1)} %fusion.22), channel_id=1, source_target_pairs={{0,8},{2,10},{4,12},{6,14},{8,0},{10,2},{12,4},{14,6},{1,9},{3,11}... | collective-permute-start | bytes 12296 | tf_op jit(solution)/shard_map/ppermute | solution.py:23
  60.6 0.9 copy-start.4
  62.2 10.1 %collective-permute-start.3 = (f32[2,4,90,128]{3,2,1,0:T(8,128)}, f32[2,4,90,128]{3,2,1,0:T(8,128)}, u32[]{:S(2)}, u32[]{:S(2)}) collective-permute-start(f32[2,4,90,128]{3,2,1,0:T(8,128)} %constant_dynamic-slice_fusion.6), channel_id=1, source_target_pairs={{0,1},{1,0},{2,3},{3,2},{4,5},{5,4},{6,7},{7,6},{8,9},{9,8},{10,11... | collective-permute-start | bytes 1105928 | tf_op jit(solution)/shard_map/ppermute | solution.py:144
  74.6 3.6 %collective-permute-start.4 = (f32[2,128]{1,0:T(2,128)S(1)}, f32[2,128]{1,0:T(2,128)S(1)}, u32[]{:S(2)}, u32[]{:S(2)}) collective-permute-start(f32[2,128]{1,0:T(2,128)S(1)} %pad_maximum_fusion.4), channel_id=1, source_target_pairs={{0,2},{2,0},{4,6},{6,4},{8,10},{10,8},{12,14},{14,12},{1,3},{3,1},... | collective-permute-start | bytes 3080 | tf_op jit(solution)/shard_map/ppermute | solution.py:23
  78.2 3.6 %collective-permute-start.5 = (f32[2,128]{1,0:T(2,128)S(1)}, f32[2,128]{1,0:T(2,128)S(1)}, u32[]{:S(2)}, u32[]{:S(2)}) collective-permute-start(f32[2,128]{1,0:T(2,128)S(1)} %fusion.7), channel_id=1, source_target_pairs={{0,4},{2,6},{4,0},{6,2},{8,12},{10,14},{12,8},{14,10},{1,5},{3,7},... | collective-permute-start | bytes 3080 | tf_op jit(solution)/shard_map/ppermute | solution.py:23
  81.9 4.5 %collective-permute-start.6 = (f32[2,128]{1,0:T(2,128)S(1)}, f32[2,128]{1,0:T(2,128)S(1)}, u32[]{:S(2)}, u32[]{:S(2)}) collective-permute-start(f32[2,128]{1,0:T(2,128)S(1)} %fusion.21), channel_id=1, source_target_pairs={{0,8},{2,10},{4,12},{6,14},{8,0},{10,2},{12,4},{14,6},{1,9},{3,11}... | collective-permute-start | bytes 3080 | tf_op jit(solution)/shard_map/ppermute | solution.py:23
  109.7 51.3 %all-to-all-start = ((bf16[8,2,64,384]{3,2,1,0:T(8,128)(2,1)}), bf16[8,2,64,384]{3,2,1,0:T(8,128)(2,1)}, u32[]{:S(2)}, u32[]{:S(2)}) async-start(bf16[8,2,64,384]{3,2,1,0:T(8,128)(2,1)} %copy.133), calls=%async_computation | async-start | bytes 1572864 | tf_op jit(solution)/shard_map/all_to_all | solution.py:82
  151.9 2.2 %copy-start.1 = (bf16[8,8,90,128]{3,2,0,1:T(8,128)(2,1)}, bf16[8,8,90,128]{3,2,0,1:T(8,128)(2,1)S(1)}, u32[]{:S(2)}) copy-start(bf16[8,8,90,128]{3,2,0,1:T(8,128)(2,1)S(1)} %copy.126) | copy-start | bytes 4423684
  153.5 1.5 copy-start.12
  154.9 4.0 %copy-start.10 = (f32[32,1]{0,1:T(1,128)S(1)}, f32[32,1]{0,1:T(1,128)}, u32[]{:S(2)}) copy-start(f32[32,1]{0,1:T(1,128)} %get-tuple-element.50) | copy-start | bytes 388
  154.9 4.7 %copy-start.5 = (f32[256]{0:T(256)S(1)}, f32[256]{0:T(256)}, u32[]{:S(2)}) copy-start(f32[256]{0:T(256)} %reshape.341) | copy-start | bytes 3076
  154.9 4.7 %copy-start.6 = (f32[256]{0:T(256)S(1)}, f32[256]{0:T(256)}, u32[]{:S(2)}) copy-start(f32[256]{0:T(256)} %reshape.343) | copy-start | bytes 3076
  154.9 12.0 %copy-start.7 = (f32[128]{0:T(128)S(1)}, f32[128]{0:T(128)}, u32[]{:S(2)}) copy-start(f32[128]{0:T(128)} %fusion.5) | copy-start | bytes 1540
  158.1 8.8 %collective-permute-start.7 = (f32[2,4,90,128]{3,2,1,0:T(8,128)}, f32[2,4,90,128]{3,2,1,0:T(8,128)}, u32[]{:S(2)}, u32[]{:S(2)}) collective-permute-start(f32[2,4,90,128]{3,2,1,0:T(8,128)} %copy.146), channel_id=1, source_target_pairs={{0,1},{1,0},{2,3},{3,2},{4,5},{5,4},{6,7},{7,6},{8,9},{9,8},{10,11... | collective-permute-start | bytes 1105928 | tf_op jit(solution)/shard_map/ppermute | solution.py:144
  169.2 5.5 %collective-permute-start.8 = (f32[2,128]{1,0:T(2,128)S(1)}, f32[2,128]{1,0:T(2,128)S(1)}, u32[]{:S(2)}, u32[]{:S(2)}) collective-permute-start(f32[2,128]{1,0:T(2,128)S(1)} %pad_maximum_fusion.5), channel_id=1, source_target_pairs={{0,2},{2,0},{4,6},{6,4},{8,10},{10,8},{12,14},{14,12},{1,3},{3,1},... | collective-permute-start | bytes 3080 | tf_op jit(solution)/shard_map/ppermute | solution.py:23
  174.7 11.9 %copy-start.2 = (bf16[8,8,90,128]{3,2,0,1:T(8,128)(2,1)S(1)}, bf16[8,8,90,128]{3,2,0,1:T(8,128)(2,1)}, u32[]{:S(2)}) copy-start(bf16[8,8,90,128]{3,2,0,1:T(8,128)(2,1)} %copy-done.1) | copy-start | bytes 4423684
  174.7 13.9 %collective-permute-start.9 = (f32[2,128]{1,0:T(2,128)S(1)}, f32[2,128]{1,0:T(2,128)S(1)}, u32[]{:S(2)}, u32[]{:S(2)}) collective-permute-start(f32[2,128]{1,0:T(2,128)S(1)} %fusion.6), channel_id=1, source_target_pairs={{0,4},{2,6},{4,0},{6,2},{8,12},{10,14},{12,8},{14,10},{1,5},{3,7},... | collective-permute-start | bytes 3080 | tf_op jit(solution)/shard_map/ppermute | solution.py:23
  186.7 14.2 %copy-start.3 = (f32[2,4,90,256]{3,2,1,0:T(8,128)S(1)}, f32[2,4,90,256]{3,2,1,0:T(8,128)}, u32[]{:S(2)}) copy-start(f32[2,4,90,256]{3,2,1,0:T(8,128)} %get-tuple-element.39) | copy-start | bytes 2211844
  186.7 14.2 %copy-start.8 = (f32[128]{0:T(128)S(1)}, f32[128]{0:T(128)}, u32[]{:S(2)}) copy-start(f32[128]{0:T(128)} %fusion.5) | copy-start | bytes 1540
  186.7 14.2 %copy-start.9 = (f32[128]{0:T(128)S(1)}, f32[128]{0:T(128)}, u32[]{:S(2)}) copy-start(f32[128]{0:T(128)} %dynamic_slice.80) | copy-start | bytes 1540
  188.6 14.3 %copy-start.11 = (f32[1,128]{1,0:T(1,128)S(1)}, f32[1,128]{1,0:T(1,128)}, u32[]{:S(2)}) copy-start(f32[1,128]{1,0:T(1,128)} %get-tuple-element.45) | copy-start | bytes 1540
  188.6 11.6 %collective-permute-start.10 = (f32[2,128]{1,0:T(2,128)S(1)}, f32[2,128]{1,0:T(2,128)S(1)}, u32[]{:S(2)}, u32[]{:S(2)}) collective-permute-start(f32[2,128]{1,0:T(2,128)S(1)} %fusion.20), channel_id=1, source_target_pairs={{0,8},{2,10},{4,12},{6,14},{8,0},{10,2},{12,4},{14,6},{1,9},{3,11}... | collective-permute-start | bytes 3080 | tf_op jit(solution)/shard_map/ppermute | solution.py:23
Sparse Core Ops, SparseCore 0:
  17.9 36.9 all-gather.2
  99.2 51.0 all-gather.4

commit v2 on v1

v2 whole, which is shorter than its diff:
```python
import jax
import jax.numpy as jnp
from jax import lax
from jax.experimental import pallas as pl
from jax.experimental.pallas import tpu as pltpu
from jax.sharding import PartitionSpec as P

GROUPS = 32


epsilon = 1e-06


CLIP = ("tm", "space")


def clip_totals(values):
    count = lax.axis_size(CLIP)
    if count & (count - 1):
        return lax.psum(values, CLIP)
    step = 1
    while step < count:
        values = values + lax.ppermute(values, CLIP, [(i, i ^ step) for i in range(count)])
        step *= 2
    return values


def group_sums(values, per):
    group = jnp.arange(values.shape[1]) // per
    same = (group[:, None] == group[None, :]).astype(jnp.float32)
    return jnp.dot(values, same, precision=lax.Precision.HIGHEST)


def norm_back(upstream, centred, scaled, gain, scale, members, per):
    gate = jax.nn.sigmoid(scaled)
    slope = upstream * gate * (1.0 + scaled * (1.0 - gate))
    totals = clip_totals(
        jnp.stack([jnp.sum(slope, axis=(0, 1, 2)), jnp.sum(slope * centred, axis=(0, 1, 2))])
    )
    shifts = group_sums(gain * totals, per) / members
    return (scale * (slope * gain - shifts[0] - centred * shifts[1]), totals[1])


def tap_stack(extended, frames, height, width):
    pieces = []
    for frame_tap in range(3):
        for row_tap in range(3):
            for col_tap in range(3):
                pieces.append(
                    extended[
                        2 - frame_tap : 2 - frame_tap + frames,
                        2 - row_tap : 2 - row_tap + height,
                        2 - col_tap : 2 - col_tap + width,
                    ]
                )
    stacked = jnp.stack(pieces, axis=3)
    return stacked.reshape(frames * height * width, 27, extended.shape[3])


def rounded_up(size, unit):
    return -(-size // unit) * unit


def extended(grad):
    tm, space = lax.axis_size("tm"), lax.axis_size("space")

    def moved(block, frame_step, row_step):
        route = []
        for t in range(tm):
            for s in range(space):
                if 0 <= t - frame_step and 0 <= s + row_step < space:
                    route.append((t * space + s, (t - frame_step) * space + s + row_step))
        if not route:
            return jnp.zeros_like(block)
        return lax.ppermute(block, CLIP, route)

    height = grad.shape[1]
    first, last, early = grad[:, :1], grad[:, height - 1 :], grad[:2]
    now = jnp.concatenate([moved(last, 0, 1), grad, moved(first, 0, -1)], axis=1)
    later = jnp.concatenate(
        [moved(last[:2], 1, 1), moved(early, 1, 0), moved(first[:2], 1, -1)], axis=1
    )
    joined = jnp.concatenate([now, later], axis=0)
    return jnp.pad(joined, ((0, 0), (0, 0), (1, 1), (0, 0)))


def exchanged(fields, wide, share, rows):
    kinds, frames, height, width, channels = fields.shape
    tm, space = lax.axis_size("tm"), lax.axis_size("space")
    fields = jnp.pad(fields, ((0, 0), (0, 0), (0, 0), (0, wide - width), (0, 0)))
    fields = fields.reshape(kinds, frames, height * wide, channels).transpose(0, 1, 3, 2)
    fields = fields.reshape(kinds, frames, tm * space, share, height * wide).transpose(2, 0, 1, 3, 4)
    fields = jnp.pad(fields, ((0, 0), (0, 0), (0, 0), (0, rows - share), (0, 0)))
    blocks = lax.all_to_all(fields, CLIP, 0, 0, tiled=True)
    return blocks.reshape(tm, space, kinds, frames, rows, height * wide)


def delta_share(blocks, kind, columns, grads, share, wide):
    tm, space, _, frames, rows, part = blocks.shape
    _, _, height, width, depth = grads.shape
    total, lanes = tm * frames, space * part
    tall = space * height

    def body(field_ref, columns_ref, grads_ref, out_ref, padded_ref, sum_ref):
        frame = pl.program_id(0)

        @pl.when(frame == 0)
        def _():
            sum_ref[...] = jnp.zeros_like(sum_ref)
            padded_ref[...] = jnp.zeros_like(padded_ref)
            for device in range(tm * space):
                t, s = device // space, device % space
                for f in range(frames):
                    for h in range(height):
                        row = (1 + s * height + h) * wide
                        padded_ref[t * frames + f, row : row + width, :] = grads_ref[device, f, h]

        column = columns_ref[...]
        field = jnp.concatenate([field_ref[0, s, 0, 0] for s in range(space)], axis=1)
        scaled = (field.astype(jnp.float32) - column[:, 0:1]) * column[:, 1:2] * column[:, 2:3]
        active = (scaled * jax.nn.sigmoid(scaled)).astype(jnp.bfloat16).astype(jnp.float32)
        place = lax.broadcasted_iota(jnp.int32, active.shape, 1)
        active = jnp.where(place % wide < width, active, 0.0)
        left = jnp.concatenate(
            [pltpu.roll(active, 1, 1), active, pltpu.roll(active, lanes - 1, 1)], axis=0
        ).astype(jnp.bfloat16)
        right = jnp.concatenate(
            [
                padded_ref[frame + 2 - a, (2 - b) * wide : (2 - b) * wide + lanes, :]
                for a in range(3)
                for b in range(3)
            ],
            axis=1,
        )
        sum_ref[...] += lax.dot_general(
            left, right, (((1,), (0,)), ((), ())), preferred_element_type=jnp.float32
        )

        @pl.when(frame == total - 1)
        def _():
            for a in range(3):
                for b in range(3):
                    for c in range(3):
                        column = (3 * a + b) * depth
                        out_ref[:, a, b, c, :] = sum_ref[
                            c * rows : c * rows + share, column : column + depth
                        ]

    return pl.pallas_call(
        body,
        grid=(total,),
        in_specs=[
            pl.BlockSpec(
                (1, space, 1, 1, rows, part), lambda t: (t // frames, 0, kind, t % frames, 0, 0)
            ),
            pl.BlockSpec((rows, 3), lambda t: (0, 0)),
            pl.BlockSpec(grads.shape, lambda t: (0, 0, 0, 0, 0)),
        ],
        out_specs=pl.BlockSpec((share, 3, 3, 3, depth), lambda t: (0, 0, 0, 0, 0)),
        out_shape=jax.ShapeDtypeStruct((share, 3, 3, 3, depth), jnp.float32),
        scratch_shapes=[
            pltpu.VMEM((total + 2, (tall + 2) * wide, depth), jnp.bfloat16),
            pltpu.VMEM((3 * rows, 9 * depth), jnp.float32),
        ],
        compiler_params=pltpu.CompilerParams(vmem_limit_bytes=(12 << 20) + 6 * total * tall * wide * depth),
        cost_estimate=pl.CostEstimate(
            flops=2 * total * lanes * 27 * rows * depth, bytes_accessed=4 << 20, transcendentals=0
        ),
        name="delta_share",
    )(blocks, columns, grads)


def summed_over_chan(partial, half):
    if lax.axis_size("chan") != 2:
        return lax.psum_scatter(partial, "chan", scatter_dimension=3, tiled=True)
    own = lax.axis_index("chan") * half
    other = lax.ppermute(
        lax.dynamic_slice_in_dim(partial, half - own, half, 3), "chan", [(0, 1), (1, 0)]
    )
    return lax.dynamic_slice_in_dim(partial, own, half, 3) + other


def gradient_back(grad, kernel, shape):
    frames, height, width, channels = shape
    half = kernel.shape[4]
    taps = tap_stack(extended(grad), frames, height, width)
    partial = lax.dot_general(
        taps,
        kernel.reshape(channels, 27, half),
        (((1, 2), (1, 2)), ((), ())),
        preferred_element_type=jnp.float32,
    )
    return summed_over_chan(partial.reshape(frames, height, width, channels), half)


def shards(features, hidden, cotangent, kernel_one, kernel_two, gains):
    frames, height, width, channels = features.shape
    half = kernel_one.shape[4]
    per = channels // GROUPS
    offset = lax.axis_index("chan") * half
    members = float(frames * height * width * per * lax.axis_size(CLIP))
    share = channels // lax.axis_size(CLIP)
    rows = rounded_up(share, 8)
    wide = rounded_up(width, 32)

    def own(field):
        return lax.dynamic_slice_in_dim(field, offset, half, field.ndim - 1)

    def shared(mean, scale, gain):
        values = jnp.stack([mean, scale, gain])
        values = lax.dynamic_slice_in_dim(values, lax.axis_index(CLIP) * share, share, 1)
        return jnp.pad(values.T, ((0, rows - share), (0, 0)))

    cotangent_own = own(cotangent)
    grads_two = lax.all_gather(cotangent_own, CLIP)
    both = exchanged(jnp.stack([features, hidden]), wide, share, rows)
    field_one = features.astype(jnp.float32)
    field_two = hidden.astype(jnp.float32)
    totals = clip_totals(
        jnp.stack(
            [
                jnp.sum(field_one, axis=(0, 1, 2)),
                jnp.sum(field_two, axis=(0, 1, 2)),
                jnp.sum(field_one * field_one, axis=(0, 1, 2)),
                jnp.sum(field_two * field_two, axis=(0, 1, 2)),
            ]
        )
    )
    moments = group_sums(totals, per) / members
    means = moments[:2]
    scales = lax.rsqrt(moments[2:] - means * means + epsilon)
    centred_one = (own(field_one) - own(means[0])) * own(scales[0])
    scaled_one = centred_one * own(gains[0])
    centred_two = (own(field_two) - own(means[1])) * own(scales[1])
    scaled_two = centred_two * own(gains[1])
    back_two = gradient_back(cotangent_own, kernel_two, features.shape)
    grad_two, weighted_two = norm_back(
        back_two, centred_two, scaled_two, own(gains[1]), own(scales[1]), members, per
    )
    grad_hidden = grad_two.astype(jnp.bfloat16)
    grads_one = lax.all_gather(grad_hidden, CLIP)
    delta_two = delta_share(
        both, 1, shared(means[1], scales[1], gains[1]), grads_two, share, wide
    )
    back_one = gradient_back(grad_hidden, kernel_one, features.shape)
    grad_one, weighted_one = norm_back(
        back_one, centred_one, scaled_one, own(gains[0]), own(scales[0]), members, per
    )
    delta_one = delta_share(
        both, 0, shared(means[0], scales[0], gains[0]), grads_one, share, wide
    )
    feature_grad = (cotangent_own.astype(jnp.float32) + grad_one).astype(jnp.bfloat16)
    return (feature_grad, delta_one, delta_two, jnp.stack([weighted_one, weighted_two]))


def solution(mesh):
    placed = (
        P(("clip", "tm"), "space", None, None),
        P(("clip", "tm"), "space", None, None),
        P(("clip", "tm"), "space", None, None),
        P(None, None, None, None, "chan"),
        P(None, None, None, None, "chan"),
        P(),
    )
    return jax.shard_map(
        shards,
        mesh=mesh,
        in_specs=placed,
        out_specs=(
            P(("clip", "tm"), "space", None, "chan"),
            P(("clip", "tm", "space"), None, None, None, "chan"),
            P(("clip", "tm", "space"), None, None, None, "chan"),
            P("clip", "chan"),
        ),
        check_vma=False,
    )
```

time: 212 us -> 155 us (0.73)
  local copies, waits for them, and re-layouts: 55.2 us -> 18.1 us
  starting transfers between devices: 17.6 us -> 44.9 us
  waiting for transfers between devices: 66.5 us -> 46.7 us
  blocking collectives: 14.9 us -> 0 us
  other arithmetic: 22.6 us -> 11.1 us
    all_gather x2, waiting for transfers between devices: 57 us -> 0.01 us  [the longest x1 0.01 us: shards(): grads_two = lax.all_gather(cotangent_own, CLIP)]
    ppermute x9, waiting for transfers between devices: 9.48 us -> 32.9 us  [clip_totals(): lax.ppermute(values, CLIP, [(i, i ^ step) for i in range(count)])]
    ppermute x0 -> x10, starting transfers between devices: none -> 17.5 us  [moved(): return lax.ppermute(block, CLIP, route)]
    all_gather x2 -> x0, blocking collectives: 14.9 us -> none  [gathered(): rows = lax.all_gather(grad, 'space', axis=1, tiled=True)]
    ppermute x0 -> x10, waiting for transfers between devices: none -> 12.1 us  [moved(): return lax.ppermute(block, CLIP, route)]
    reshape x7 -> x0, local copies, waits for them, and re-layouts: 7.8 us -> none  [the longest x2 3.17 us: delta_share(): return out.reshape(3, rows, 3, 3, depth).transpose(1, 2, 3, 0, 4)]
    ppermute x9, starting transfers between devices: 13.2 us -> 20.4 us  [clip_totals(): lax.ppermute(values, CLIP, [(i, i ^ step) for i in range(count)])]
    pad x4 -> x0, local copies, waits for them, and re-layouts: 6.22 us -> none  [the longest x2 3.65 us: gathered(): return jnp.pad(whole, ((0, 2), (1, 1), (0, wide - grad.shape[2]), (0, 0)))]
  transfers between devices with their start and end apart: 14 -> 24, of which waited for: 6 -> 12; matrix products, arithmetic and copies ran while one was open for 30% -> 19% of each run, Pallas kernels for 7% -> 5%
where the time goes in v2:
time: 155 us; the launch traced here: 153 us
  waiting for transfers between devices  46.7 us (30%)
  starting transfers between devices  44.9 us (29%)
  local copies, waits for them, and re-layouts  18.1 us (12%)
  between operations  14.6 us (9%)
  Pallas kernels  13.8 us (9%)
  other arithmetic  11.1 us (7%)
  matrix products  3.86 us (2%)
    ppermute x9, waiting for transfers between devices, clip_totals(): lax.ppermute(values, CLIP, [(i, i ^ step) for i in range(count)])  32.9 us
    ppermute x9, starting transfers between devices, clip_totals(): lax.ppermute(values, CLIP, [(i, i ^ step) for i in range(count)])  20.4 us
    ppermute x10, starting transfers between devices, moved(): return lax.ppermute(block, CLIP, route)  17.5 us
    pallas_call x2, Pallas kernels, delta_share(): pl.pallas_call(body, grid=(total,), in_specs=[pl.BlockSpec((1, space, 1,...  13.8 us
    ppermute x10, waiting for transfers between devices, moved(): return lax.ppermute(block, CLIP, route)  12.1 us
    unnamed x73, local copies, waits for them, and re-layouts  7.04 us
    all_to_all x1, starting transfers between devices, exchanged(): blocks = lax.all_to_all(fields, CLIP, 0, 0, tiled=True)  6.87 us
    dot_general x2, matrix products, gradient_back(): lax.dot_general(taps, kernel.reshape(channels, 27, half), (((1, 2), (1, 2...  3.23 us
  transfers between devices with their start and end apart: 24, of which 12 were waited for; matrix products, arithmetic and copies ran while one was open for 19% of the time, Pallas kernels for 5%

profile of v2, /device:TPU:0, one launch (start us, length us, event | category | flops | bytes accessed | tf_op | source)
XLA Modules:
  0.0 153.2 jit_solution(8621885910585556870)
XLA Ops:
  7.2 1.1 constant_dynamic-slice_fusion.15
  8.4 1.3 collective-permute-start.6
  10.3 5.5 %collective-permute-start.3 = (bf16[2,1,90,128]{3,2,1,0:T(8,128)(2,1)}, bf16[2,1,90,128]{3,2,1,0:T(8,128)(2,1)}, u32[]{:S(2)}, u32[]{:S(2)}) collective-permute-start(bf16[2,1,90,128]{3,2,1,0:T(8,128)(2,1)} %get-tuple-element.34), channel_id=1, source_target_pairs={{0,2},{4,6},{8,10},{12,14},{1,3},{5,7},{9,11},{13,15},{16,18},{20,... | collective-permute-start | bytes 138248 | tf_op jit(solution)/shard_map/ppermute | solution.py:75
  15.8 1.3 collective-permute-start.5
  17.2 1.3 collective-permute-start.4
  18.5 1.1 convert_reduce_fusion.1
  19.6 1.1 convert_reduce_fusion
  20.8 2.7 %collective-permute-start = (f32[4,256]{1,0:T(4,128)S(1)}, f32[4,256]{1,0:T(4,128)S(1)}, u32[]{:S(2)}, u32[]{:S(2)}) collective-permute-start(f32[4,256]{1,0:T(4,128)S(1)} %pad_maximum_fusion.8), channel_id=1, source_target_pairs={{0,2},{2,0},{4,6},{6,4},{8,10},{10,8},{12,14},{14,12},{1,3},{3,1},... | collective-permute-start | bytes 12296 | tf_op jit(solution)/shard_map/ppermute | solution.py:23
  23.5 1.1 copy_bitcast_fusion
  25.3 3.3 %collective-permute-start.1 = (f32[4,256]{1,0:T(4,128)S(1)}, f32[4,256]{1,0:T(4,128)S(1)}, u32[]{:S(2)}, u32[]{:S(2)}) collective-permute-start(f32[4,256]{1,0:T(4,128)S(1)} %fusion.61), channel_id=1, source_target_pairs={{0,4},{2,6},{4,0},{6,2},{8,12},{10,14},{12,8},{14,10},{1,5},{3,7},... | collective-permute-start | bytes 12296 | tf_op jit(solution)/shard_map/ppermute | solution.py:23
  28.7 1.6 %collective-permute-done.1 = f32[4,256]{1,0:T(4,128)S(1)} collective-permute-done((f32[4,256]{1,0:T(4,128)S(1)}, f32[4,256]{1,0:T(4,128)S(1)}, u32[]{:S(2)}, u32[]{:S(2)}) %collective-permute-start.1) | collective-permute-done | bytes 4128 | tf_op jit(solution)/shard_map/ppermute | solution.py:23
  30.3 3.1 %collective-permute-start.2 = (f32[4,256]{1,0:T(4,128)S(1)}, f32[4,256]{1,0:T(4,128)S(1)}, u32[]{:S(2)}, u32[]{:S(2)}) collective-permute-start(f32[4,256]{1,0:T(4,128)S(1)} %fusion.75), channel_id=1, source_target_pairs={{0,8},{2,10},{4,12},{6,14},{8,0},{10,2},{12,4},{14,6},{1,9},{3,11}... | collective-permute-start | bytes 12296 | tf_op jit(solution)/shard_map/ppermute | solution.py:23
  33.4 1.7 %collective-permute-done.2 = f32[4,256]{1,0:T(4,128)S(1)} collective-permute-done((f32[4,256]{1,0:T(4,128)S(1)}, f32[4,256]{1,0:T(4,128)S(1)}, u32[]{:S(2)}, u32[]{:S(2)}) %collective-permute-start.2) | collective-permute-done | bytes 4128 | tf_op jit(solution)/shard_map/ppermute | solution.py:23
  35.1 1.3 collective-permute-start.7
  36.7 5.5 %collective-permute-done.7 = bf16[2,1,90,128]{3,2,1,0:T(8,128)(2,1)S(1)} collective-permute-done((bf16[2,1,90,128]{3,2,1,0:T(8,128)(2,1)}, bf16[2,1,90,128]{3,2,1,0:T(8,128)(2,1)S(1)}, u32[]{:S(2)}, u32[]{:S(2)}) %collective-permute-start.7) | collective-permute-done | bytes 46112 | tf_op jit(solution)/shard_map/ppermute | solution.py:75
  42.2 0.9 maximum_maximum_fusion
  43.6 0.9 fusion.30
  45.6 0.8 fusion.23
  46.5 1.6 %convolution_bitcast_fusion = f32[2,4,90,256]{3,2,1,0:T(8,128)S(1)} fusion(bf16[2,4,90,27,128]{4,2,3,1,0:T(8,128)(2,1)S(1)} %bitcast_dynamic-update-slice_fusion.38, bf16[256,27,128,1,1]{2,0,1,4,3:T(8,128)(2,1)S(1)} %bitcast.247), kind=kOutput, calls=%fused_computation.6 | convolution fusion | flops 1274019840 | bytes 7483392 | tf_op jit(solution)/shard_map/dot_general | solution.py:187
  48.3 1.7 %collective-permute-done.8 = f32[2,4,90,128]{3,2,1,0:T(8,128)S(1)} collective-permute-done((f32[2,4,90,128]{3,2,1,0:T(8,128)S(1)}, f32[2,4,90,128]{3,2,1,0:T(8,128)S(1)}, u32[]{:S(2)}, u32[]{:S(2)}) %collective-permute-start.8) | collective-permute-done | bytes 368672 | tf_op jit(solution)/shard_map/ppermute | solution.py:177
  50.3 3.7 %collective-permute-done.9 = f32[2,128]{1,0:T(2,128)S(1)} collective-permute-done((f32[2,128]{1,0:T(2,128)S(1)}, f32[2,128]{1,0:T(2,128)S(1)}, u32[]{:S(2)}, u32[]{:S(2)}) %collective-permute-start.9) | collective-permute-done | bytes 1056 | tf_op jit(solution)/shard_map/ppermute | solution.py:23
  54.0 1.9 %collective-permute-start.10 = (f32[2,128]{1,0:T(2,128)S(1)}, f32[2,128]{1,0:T(2,128)S(1)}, u32[]{:S(2)}, u32[]{:S(2)}) collective-permute-start(f32[2,128]{1,0:T(2,128)S(1)} %fusion.60), channel_id=1, source_target_pairs={{0,4},{2,6},{4,0},{6,2},{8,12},{10,14},{12,8},{14,10},{1,5},{3,7},... | collective-permute-start | bytes 3080 | tf_op jit(solution)/shard_map/ppermute | solution.py:23
  55.9 1.7 %collective-permute-done.10 = f32[2,128]{1,0:T(2,128)S(1)} collective-permute-done((f32[2,128]{1,0:T(2,128)S(1)}, f32[2,128]{1,0:T(2,128)S(1)}, u32[]{:S(2)}, u32[]{:S(2)}) %collective-permute-start.10) | collective-permute-done | bytes 1056 | tf_op jit(solution)/shard_map/ppermute | solution.py:23
  57.7 2.9 %collective-permute-start.11 = (f32[2,128]{1,0:T(2,128)S(1)}, f32[2,128]{1,0:T(2,128)S(1)}, u32[]{:S(2)}, u32[]{:S(2)}) collective-permute-start(f32[2,128]{1,0:T(2,128)S(1)} %fusion.74), channel_id=1, source_target_pairs={{0,8},{2,10},{4,12},{6,14},{8,0},{10,2},{12,4},{14,6},{1,9},{3,11}... | collective-permute-start | bytes 3080 | tf_op jit(solution)/shard_map/ppermute | solution.py:23
  60.6 1.7 %collective-permute-done.11 = f32[2,128]{1,0:T(2,128)S(1)} collective-permute-done((f32[2,128]{1,0:T(2,128)S(1)}, f32[2,128]{1,0:T(2,128)S(1)}, u32[]{:S(2)}, u32[]{:S(2)}) %collective-permute-start.11) | collective-permute-done | bytes 1056 | tf_op jit(solution)/shard_map/ppermute | solution.py:23
  63.0 1.3 collective-permute-start.15
  64.3 2.3 %collective-permute-start.12 = (bf16[2,1,90,128]{3,2,1,0:T(8,128)(2,1)S(1)}, bf16[2,1,90,128]{3,2,1,0:T(8,128)(2,1)S(1)}, u32[]{:S(2)}, u32[]{:S(2)}) collective-permute-start(bf16[2,1,90,128]{3,2,1,0:T(8,128)(2,1)S(1)} %get-tuple-element.32), channel_id=1, source_target_pairs={{0,2},{4,6},{8,10},{12,14},{1,3},{5,7},{9,11},{13,15},{16,18},{20,... | collective-permute-start | bytes 138248 | tf_op jit(solution)/shard_map/ppermute | solution.py:75
  66.6 1.3 collective-permute-start.13
  68.6 1.3 collective-permute-start.16
  70.7 1.9 %collective-permute-done.13 = bf16[2,1,90,128]{3,2,1,0:T(8,128)(2,1)S(1)} collective-permute-done((bf16[2,1,90,128]{3,2,1,0:T(8,128)(2,1)S(1)}, bf16[2,1,90,128]{3,2,1,0:T(8,128)(2,1)S(1)}, u32[]{:S(2)}, u32[]{:S(2)}) %collective-permute-start.13) | collective-permute-done | bytes 46112 | tf_op jit(solution)/shard_map/ppermute | solution.py:75
  72.6 4.7 %collective-permute-done.16 = bf16[2,1,90,128]{3,2,1,0:T(8,128)(2,1)S(1)} collective-permute-done((bf16[2,1,90,128]{3,2,1,0:T(8,128)(2,1)S(1)}, bf16[2,1,90,128]{3,2,1,0:T(8,128)(2,1)S(1)}, u32[]{:S(2)}, u32[]{:S(2)}) %collective-permute-start.16) | collective-permute-done | bytes 46112 | tf_op jit(solution)/shard_map/ppermute | solution.py:75
  79.5 1.6 %fusion.4 = f32[2,4,90,256]{3,2,0,1:T(8,128)S(1)} fusion(bf16[256,27,128,1,1]{2,0,3,4,1:T(8,128)(2,1)S(1)} %bitcast.278, bf16[2,4,90,27,128]{4,2,1,0,3:T(8,128)(2,1)S(1)} %bitcast_dynamic-update-slice_fusion.18), kind=kOutput, calls=%fused_computation.5 | convolution fusion | flops 1274019840 | bytes 7483392 | tf_op jit(solution)/shard_map/dot_general | solution.py:187
  82.7 1.0 copy_bitcast_fusion.1
  83.8 1.2 copy.117
  85.0 2.2 %copy.118 = bf16[8,2,2,32,384]{4,3,2,1,0:T(8,128)(2,1)} copy(bf16[8,2,2,32,384]{4,3,0,2,1:T(8,128)(2,1)} %bitcast.253) | data formatting | bytes 1572864 | tf_op jit(solution)/shard_map/transpose | solution.py:92
  87.1 6.9 %all-to-all-start = ((bf16[8,2,2,32,384]{4,3,2,1,0:T(8,128)(2,1)}), bf16[8,2,2,32,384]{4,3,2,1,0:T(8,128)(2,1)}, u32[]{:S(2)}, u32[]{:S(2)}) async-start(bf16[8,2,2,32,384]{4,3,2,1,0:T(8,128)(2,1)} %copy.118), calls=%async_computation | async-start | bytes 1572864 | tf_op jit(solution)/shard_map/all_to_all | solution.py:94
  94.1 1.5 fusion.62
  95.5 2.1 %collective-permute-start.18 = (f32[2,128]{1,0:T(2,128)S(1)}, f32[2,128]{1,0:T(2,128)S(1)}, u32[]{:S(2)}, u32[]{:S(2)}) collective-permute-start(f32[2,128]{1,0:T(2,128)S(1)} %pad_maximum_fusion.10), channel_id=1, source_target_pairs={{0,2},{2,0},{4,6},{6,4},{8,10},{10,8},{12,14},{14,12},{1,3},{3,1},... | collective-permute-start | bytes 3080 | tf_op jit(solution)/shard_map/ppermute | solution.py:23
  97.6 2.3 %collective-permute-done.18 = f32[2,128]{1,0:T(2,128)S(1)} collective-permute-done((f32[2,128]{1,0:T(2,128)S(1)}, f32[2,128]{1,0:T(2,128)S(1)}, u32[]{:S(2)}, u32[]{:S(2)}) %collective-permute-start.18) | collective-permute-done | bytes 1056 | tf_op jit(solution)/shard_map/ppermute | solution.py:23
  99.9 3.1 %collective-permute-start.19 = (f32[2,128]{1,0:T(2,128)S(1)}, f32[2,128]{1,0:T(2,128)S(1)}, u32[]{:S(2)}, u32[]{:S(2)}) collective-permute-start(f32[2,128]{1,0:T(2,128)S(1)} %fusion.59), channel_id=1, source_target_pairs={{0,4},{2,6},{4,0},{6,2},{8,12},{10,14},{12,8},{14,10},{1,5},{3,7},... | collective-permute-start | bytes 3080 | tf_op jit(solution)/shard_map/ppermute | solution.py:23
  103.1 8.2 %collective-permute-done.19 = f32[2,128]{1,0:T(2,128)S(1)} collective-permute-done((f32[2,128]{1,0:T(2,128)S(1)}, f32[2,128]{1,0:T(2,128)S(1)}, u32[]{:S(2)}, u32[]{:S(2)}) %collective-permute-start.19) | collective-permute-done | bytes 1056 | tf_op jit(solution)/shard_map/ppermute | solution.py:23
  111.3 1.2 collective-permute-start.20
  112.8 12.0 %collective-permute-done.20 = f32[2,128]{1,0:T(2,128)S(1)} collective-permute-done((f32[2,128]{1,0:T(2,128)S(1)}, f32[2,128]{1,0:T(2,128)S(1)}, u32[]{:S(2)}, u32[]{:S(2)}) %collective-permute-start.20) | collective-permute-done | bytes 1056 | tf_op jit(solution)/shard_map/ppermute | solution.py:23
  125.0 1.2 add_convert_fusion
  127.5 1.7 %copy.124 = bf16[16,4,90,128]{3,2,1,0:T(8,128)(2,1)S(1)} copy(bf16[16,4,90,128]{3,1,2,0:T(4,128)(2,1)} %all-gather.7.cloned.1.call-done) | data formatting | bytes 2949120 | tf_op jit(solution)/shard_map/all_gather | solution.py:215
  129.2 6.9 %delta_share.3 = f32[32,3,3,3,128]{4,3,2,1,0:T(4,128)S(1)} custom-call(bf16[4,2,2,2,32,384]{5,4,3,2,1,0:T(8,128)(2,1)} %bitcast.112.field_ref, f32[32,3]{1,0:T(8,128)S(1)} %bitcast.251, bf16[8,2,4,90,128]{4,3,2,1,0:T(8,128)(2,1)S(1)} %bitcast.248), custom_call_target="tpu_custom_call" | custom-call | flops 1358954496 | bytes 4194304 | tf_op jit(solution)/shard_map/delta_share/pallas_call | solution.py:149
  136.9 1.7 %copy.121 = bf16[16,4,90,128]{3,2,1,0:T(8,128)(2,1)S(1)} copy(bf16[16,4,90,128]{3,1,2,0:T(4,128)(2,1)} %all-gather.5.cloned.1.call-done) | data formatting | bytes 2949120 | tf_op jit(solution)/shard_map/all_gather | solution.py:241
  138.6 6.9 %delta_share.2 = f32[32,3,3,3,128]{4,3,2,1,0:T(4,128)S(1)} custom-call(bf16[4,2,2,2,32,384]{5,4,3,2,1,0:T(8,128)(2,1)} %bitcast.112.field_ref, f32[32,3]{1,0:T(8,128)S(1)} %bitcast.250, bf16[8,2,4,90,128]{4,3,2,1,0:T(8,128)(2,1)S(1)} %bitcast.249), custom_call_target="tpu_custom_call" | custom-call | flops 1358954496 | bytes 4194304 | tf_op jit(solution)/shard_map/delta_share/pallas_call | solution.py:149
  (140 shorter events, 13.4 us)
Async XLA Ops:
  7.2 39.3 %copy-start = (bf16[256,3,3,3,128]{4,0,3,2,1:T(8,128)(2,1)S(1)}, bf16[256,3,3,3,128]{4,0,3,2,1:T(8,128)(2,1)}, u32[]{:S(2)}) copy-start(bf16[256,3,3,3,128]{4,0,3,2,1:T(8,128)(2,1)} %param.10) | copy-start | bytes 5308420
  7.2 120.3 %all-gather.7.cloned.1.call-start = ((), (), s32[]{:S(2)}) async-start(), calls=%async_computation.2 | async-start | bytes 1658880 | tf_op jit(solution)/shard_map/all_gather | solution.py:215
  8.3 8.7 %copy-start.1 = (bf16[2,4,90,128]{3,1,2,0:T(4,128)(2,1)}, bf16[2,4,90,128]{3,1,2,0:T(4,128)(2,1)S(1)}, u32[]{:S(2)}) copy-start(bf16[2,4,90,128]{3,1,2,0:T(4,128)(2,1)S(1)} %constant_dynamic-slice_fusion.15) | copy-start | bytes 552964
  8.4 33.8 %collective-permute-start.6 = (bf16[2,4,90,128]{3,2,1,0:T(8,128)(2,1)S(1)}, bf16[2,4,90,128]{3,2,1,0:T(8,128)(2,1)S(1)}, u32[]{:S(2)}, u32[]{:S(2)}) collective-permute-start(bf16[2,4,90,128]{3,2,1,0:T(8,128)(2,1)S(1)} %copy.131), channel_id=1, source_target_pairs={{4,0},{6,2},{8,4},{10,6},{12,8},{14,10},{5,1},{7,3},{9,5},{11,7},{... | collective-permute-start | bytes 552968 | tf_op jit(solution)/shard_map/ppermute | solution.py:75
  10.3 26.3 %collective-permute-start.3 = (bf16[2,1,90,128]{3,2,1,0:T(8,128)(2,1)}, bf16[2,1,90,128]{3,2,1,0:T(8,128)(2,1)}, u32[]{:S(2)}, u32[]{:S(2)}) collective-permute-start(bf16[2,1,90,128]{3,2,1,0:T(8,128)(2,1)} %get-tuple-element.34), channel_id=1, source_target_pairs={{0,2},{4,6},{8,10},{12,14},{1,3},{5,7},{9,11},{13,15},{16,18},{20,... | collective-permute-start | bytes 138248 | tf_op jit(solution)/shard_map/ppermute | solution.py:75
  15.8 20.9 %collective-permute-start.5 = (bf16[2,1,90,128]{3,2,1,0:T(8,128)(2,1)}, bf16[2,1,90,128]{3,2,1,0:T(8,128)(2,1)}, u32[]{:S(2)}, u32[]{:S(2)}) collective-permute-start(bf16[2,1,90,128]{3,2,1,0:T(8,128)(2,1)} %get-tuple-element.34), channel_id=1, source_target_pairs={{4,2},{8,6},{12,10},{5,3},{9,7},{13,11},{20,18},{24,22},{28,26},{2... | collective-permute-start | bytes 138248 | tf_op jit(solution)/shard_map/ppermute | solution.py:75
  17.1 119.8 %all-gather.5.cloned.1.call-start = ((), (), s32[]{:S(2)}) async-start(), calls=%async_computation.1 | async-start | bytes 1658880 | tf_op jit(solution)/shard_map/all_gather | solution.py:241
  17.2 19.5 %collective-permute-start.4 = (bf16[2,1,90,128]{3,2,1,0:T(8,128)(2,1)}, bf16[2,1,90,128]{3,2,1,0:T(8,128)(2,1)S(1)}, u32[]{:S(2)}, u32[]{:S(2)}) collective-permute-start(bf16[2,1,90,128]{3,2,1,0:T(8,128)(2,1)} %get-tuple-element.35), channel_id=1, source_target_pairs={{2,0},{6,4},{10,8},{14,12},{3,1},{7,5},{11,9},{15,13},{18,16},{22,... | collective-permute-start | bytes 138248 | tf_op jit(solution)/shard_map/ppermute | solution.py:75
  20.8 4.6 %collective-permute-start = (f32[4,256]{1,0:T(4,128)S(1)}, f32[4,256]{1,0:T(4,128)S(1)}, u32[]{:S(2)}, u32[]{:S(2)}) collective-permute-start(f32[4,256]{1,0:T(4,128)S(1)} %pad_maximum_fusion.8), channel_id=1, source_target_pairs={{0,2},{2,0},{4,6},{6,4},{8,10},{10,8},{12,14},{14,12},{1,3},{3,1},... | collective-permute-start | bytes 12296 | tf_op jit(solution)/shard_map/ppermute | solution.py:23
  25.3 4.9 %collective-permute-start.1 = (f32[4,256]{1,0:T(4,128)S(1)}, f32[4,256]{1,0:T(4,128)S(1)}, u32[]{:S(2)}, u32[]{:S(2)}) collective-permute-start(f32[4,256]{1,0:T(4,128)S(1)} %fusion.61), channel_id=1, source_target_pairs={{0,4},{2,6},{4,0},{6,2},{8,12},{10,14},{12,8},{14,10},{1,5},{3,7},... | collective-permute-start | bytes 12296 | tf_op jit(solution)/shard_map/ppermute | solution.py:23
  30.3 4.8 %collective-permute-start.2 = (f32[4,256]{1,0:T(4,128)S(1)}, f32[4,256]{1,0:T(4,128)S(1)}, u32[]{:S(2)}, u32[]{:S(2)}) collective-permute-start(f32[4,256]{1,0:T(4,128)S(1)} %fusion.75), channel_id=1, source_target_pairs={{0,8},{2,10},{4,12},{6,14},{8,0},{10,2},{12,4},{14,6},{1,9},{3,11}... | collective-permute-start | bytes 12296 | tf_op jit(solution)/shard_map/ppermute | solution.py:23
  35.1 7.1 %collective-permute-start.7 = (bf16[2,1,90,128]{3,2,1,0:T(8,128)(2,1)}, bf16[2,1,90,128]{3,2,1,0:T(8,128)(2,1)S(1)}, u32[]{:S(2)}, u32[]{:S(2)}) collective-permute-start(bf16[2,1,90,128]{3,2,1,0:T(8,128)(2,1)} %get-tuple-element.35), channel_id=1, source_target_pairs={{6,0},{10,4},{14,8},{7,1},{11,5},{15,9},{22,16},{26,20},{30,24},{2... | collective-permute-start | bytes 138248 | tf_op jit(solution)/shard_map/ppermute | solution.py:75
  36.7 6.7 %copy-start.4 = (bf16[2,1,90,128]{3,2,1,0:T(8,128)(2,1)}, bf16[2,1,90,128]{3,2,1,0:T(8,128)(2,1)S(1)}, u32[]{:S(2)}) copy-start(bf16[2,1,90,128]{3,2,1,0:T(8,128)(2,1)S(1)} %collective-permute-done.4) | copy-start | bytes 138244
  43.5 1.7 %copy-start.5 = (bf16[2,1,90,128]{3,2,1,0:T(8,128)(2,1)S(1)}, bf16[2,1,90,128]{3,2,1,0:T(8,128)(2,1)}, u32[]{:S(2)}) copy-start(bf16[2,1,90,128]{3,2,1,0:T(8,128)(2,1)} %copy-done.4) | copy-start | bytes 138244
  43.5 1.9 %copy-start.2 = (bf16[2,4,90,128]{3,1,2,0:T(4,128)(2,1)S(1)}, bf16[2,4,90,128]{3,1,2,0:T(4,128)(2,1)}, u32[]{:S(2)}) copy-start(bf16[2,4,90,128]{3,1,2,0:T(4,128)(2,1)} %copy-done.1) | copy-start | bytes 552964
  48.2 1.8 %collective-permute-start.8 = (f32[2,4,90,128]{3,2,1,0:T(8,128)S(1)}, f32[2,4,90,128]{3,2,1,0:T(8,128)S(1)}, u32[]{:S(2)}, u32[]{:S(2)}) collective-permute-start(f32[2,4,90,128]{3,2,1,0:T(8,128)S(1)} %constant_dynamic-slice_fusion.12), channel_id=1, source_target_pairs={{0,1},{1,0},{2,3},{3,2},{4,5},{5,4},{6,7},{7,6},{8,9},{9,8},{10,11... | collective-permute-start | bytes 1105928 | tf_op jit(solution)/shard_map/ppermute | solution.py:177
  50.2 3.8 %collective-permute-start.9 = (f32[2,128]{1,0:T(2,128)S(1)}, f32[2,128]{1,0:T(2,128)S(1)}, u32[]{:S(2)}, u32[]{:S(2)}) collective-permute-start(f32[2,128]{1,0:T(2,128)S(1)} %pad_maximum_fusion.9), channel_id=1, source_target_pairs={{0,2},{2,0},{4,6},{6,4},{8,10},{10,8},{12,14},{14,12},{1,3},{3,1},... | collective-permute-start | bytes 3080 | tf_op jit(solution)/shard_map/ppermute | solution.py:23
  54.0 3.6 %collective-permute-start.10 = (f32[2,128]{1,0:T(2,128)S(1)}, f32[2,128]{1,0:T(2,128)S(1)}, u32[]{:S(2)}, u32[]{:S(2)}) collective-permute-start(f32[2,128]{1,0:T(2,128)S(1)} %fusion.60), channel_id=1, source_target_pairs={{0,4},{2,6},{4,0},{6,2},{8,12},{10,14},{12,8},{14,10},{1,5},{3,7},... | collective-permute-start | bytes 3080 | tf_op jit(solution)/shard_map/ppermute | solution.py:23
  57.7 4.6 %collective-permute-start.11 = (f32[2,128]{1,0:T(2,128)S(1)}, f32[2,128]{1,0:T(2,128)S(1)}, u32[]{:S(2)}, u32[]{:S(2)}) collective-permute-start(f32[2,128]{1,0:T(2,128)S(1)} %fusion.74), channel_id=1, source_target_pairs={{0,8},{2,10},{4,12},{6,14},{8,0},{10,2},{12,4},{14,6},{1,9},{3,11}... | collective-permute-start | bytes 3080 | tf_op jit(solution)/shard_map/ppermute | solution.py:23
  60.6 2.0 %copy-start.9 = (s32[128]{0:T(128)}, s32[128]{0:T(128)S(1)}, u32[]{:S(2)}) copy-start(s32[128]{0:T(128)S(1)} %and_select_fusion) | copy-start | bytes 1540
  62.3 0.6 copy-start.6
  63.0 14.3 %collective-permute-start.15 = (bf16[2,4,90,128]{3,2,1,0:T(8,128)(2,1)S(1)}, bf16[2,4,90,128]{3,2,1,0:T(8,128)(2,1)S(1)}, u32[]{:S(2)}, u32[]{:S(2)}) collective-permute-start(bf16[2,4,90,128]{3,2,1,0:T(8,128)(2,1)S(1)} %multiply_convert_fusion), channel_id=1, source_target_pairs={{4,0},{6,2},{8,4},{10,6},{12,8},{14,10},{5,1},{7,3},{9,5},{11,7},{... | collective-permute-start | bytes 552968 | tf_op jit(solution)/shard_map/ppermute | solution.py:75
  64.3 6.4 %collective-permute-start.12 = (bf16[2,1,90,128]{3,2,1,0:T(8,128)(2,1)S(1)}, bf16[2,1,90,128]{3,2,1,0:T(8,128)(2,1)S(1)}, u32[]{:S(2)}, u32[]{:S(2)}) collective-permute-start(bf16[2,1,90,128]{3,2,1,0:T(8,128)(2,1)S(1)} %get-tuple-element.32), channel_id=1, source_target_pairs={{0,2},{4,6},{8,10},{12,14},{1,3},{5,7},{9,11},{13,15},{16,18},{20,... | collective-permute-start | bytes 138248 | tf_op jit(solution)/shard_map/ppermute | solution.py:75
  66.6 6.0 %collective-permute-start.13 = (bf16[2,1,90,128]{3,2,1,0:T(8,128)(2,1)S(1)}, bf16[2,1,90,128]{3,2,1,0:T(8,128)(2,1)S(1)}, u32[]{:S(2)}, u32[]{:S(2)}) collective-permute-start(bf16[2,1,90,128]{3,2,1,0:T(8,128)(2,1)S(1)} %get-tuple-element.33), channel_id=1, source_target_pairs={{2,0},{6,4},{10,8},{14,12},{3,1},{7,5},{11,9},{15,13},{18,16},{22,... | collective-permute-start | bytes 138248 | tf_op jit(solution)/shard_map/ppermute | solution.py:75
  67.9 4.7 %collective-permute-start.14 = (bf16[2,1,90,128]{3,2,1,0:T(8,128)(2,1)S(1)}, bf16[2,1,90,128]{3,2,1,0:T(8,128)(2,1)S(1)}, u32[]{:S(2)}, u32[]{:S(2)}) collective-permute-start(bf16[2,1,90,128]{3,2,1,0:T(8,128)(2,1)S(1)} %get-tuple-element.32), channel_id=1, source_target_pairs={{4,2},{8,6},{12,10},{5,3},{9,7},{13,11},{20,18},{24,22},{28,26},{2... | collective-permute-start | bytes 138248 | tf_op jit(solution)/shard_map/ppermute | solution.py:75
  68.6 8.7 %collective-permute-start.16 = (bf16[2,1,90,128]{3,2,1,0:T(8,128)(2,1)S(1)}, bf16[2,1,90,128]{3,2,1,0:T(8,128)(2,1)S(1)}, u32[]{:S(2)}, u32[]{:S(2)}) collective-permute-start(bf16[2,1,90,128]{3,2,1,0:T(8,128)(2,1)S(1)} %get-tuple-element.33), channel_id=1, source_target_pairs={{6,0},{10,4},{14,8},{7,1},{11,5},{15,9},{22,16},{26,20},{30,24},{2... | collective-permute-start | bytes 138248 | tf_op jit(solution)/shard_map/ppermute | solution.py:75
  78.0 1.5 copy-start.8
  79.5 3.2 %copy-start.3 = (bf16[2,4,90,256]{3,1,2,0:T(4,128)(2,1)S(1)}, bf16[2,4,90,256]{3,1,2,0:T(4,128)(2,1)}, u32[]{:S(2)}) copy-start(bf16[2,4,90,256]{3,1,2,0:T(4,128)(2,1)} %param.6) | copy-start | bytes 1105924
  81.9 30.8 %copy-start.7 = (f32[2,128]{1,0:T(2,128)S(1)}, f32[2,128]{1,0:T(2,128)}, u32[]{:S(2)}) copy-start(f32[2,128]{1,0:T(2,128)} %copy-done.6) | copy-start | bytes 3076
  81.9 42.8 %copy-start.10 = (s32[128]{0:T(128)S(1)}, s32[128]{0:T(128)}, u32[]{:S(2)}) copy-start(s32[128]{0:T(128)} %copy-done.9) | copy-start | bytes 1540
  82.7 11.3 %collective-permute-start.17 = (f32[2,4,90,128]{3,2,1,0:T(8,128)}, f32[2,4,90,128]{3,2,1,0:T(8,128)}, u32[]{:S(2)}, u32[]{:S(2)}) collective-permute-start(f32[2,4,90,128]{3,2,1,0:T(8,128)} %copy.133), channel_id=1, source_target_pairs={{0,1},{1,0},{2,3},{3,2},{4,5},{5,4},{6,7},{7,6},{8,9},{9,8},{10,11... | collective-permute-start | bytes 1105928 | tf_op jit(solution)/shard_map/ppermute | solution.py:177
  87.1 42.0 %all-to-all-start = ((bf16[8,2,2,32,384]{4,3,2,1,0:T(8,128)(2,1)}), bf16[8,2,2,32,384]{4,3,2,1,0:T(8,128)(2,1)}, u32[]{:S(2)}, u32[]{:S(2)}) async-start(bf16[8,2,2,32,384]{4,3,2,1,0:T(8,128)(2,1)} %copy.118), calls=%async_computation | async-start | bytes 1572864 | tf_op jit(solution)/shard_map/all_to_all | solution.py:94
  95.5 4.4 %collective-permute-start.18 = (f32[2,128]{1,0:T(2,128)S(1)}, f32[2,128]{1,0:T(2,128)S(1)}, u32[]{:S(2)}, u32[]{:S(2)}) collective-permute-start(f32[2,128]{1,0:T(2,128)S(1)} %pad_maximum_fusion.10), channel_id=1, source_target_pairs={{0,2},{2,0},{4,6},{6,4},{8,10},{10,8},{12,14},{14,12},{1,3},{3,1},... | collective-permute-start | bytes 3080 | tf_op jit(solution)/shard_map/ppermute | solution.py:23
  99.9 11.4 %collective-permute-start.19 = (f32[2,128]{1,0:T(2,128)S(1)}, f32[2,128]{1,0:T(2,128)S(1)}, u32[]{:S(2)}, u32[]{:S(2)}) collective-permute-start(f32[2,128]{1,0:T(2,128)S(1)} %fusion.59), channel_id=1, source_target_pairs={{0,4},{2,6},{4,0},{6,2},{8,12},{10,14},{12,8},{14,10},{1,5},{3,7},... | collective-permute-start | bytes 3080 | tf_op jit(solution)/shard_map/ppermute | solution.py:23
  111.3 13.4 %collective-permute-start.20 = (f32[2,128]{1,0:T(2,128)S(1)}, f32[2,128]{1,0:T(2,128)S(1)}, u32[]{:S(2)}, u32[]{:S(2)}) collective-permute-start(f32[2,128]{1,0:T(2,128)S(1)} %fusion.73), channel_id=1, source_target_pairs={{0,8},{2,10},{4,12},{6,14},{8,0},{10,2},{12,4},{14,6},{1,9},{3,11}... | collective-permute-start | bytes 3080 | tf_op jit(solution)/shard_map/ppermute | solution.py:23
Sparse Core Ops, SparseCore 0:
  17.2 45.5 all-gather.6
  70.8 57.1 all-gather.4

commit v3 on v2

--- a/solution.py
+++ b/solution.py
@@ -243,6 +243,7 @@
         both, 1, shared(means[1], scales[1], gains[1]), grads_two, share, wide
     )
     back_one = gradient_back(grad_hidden, kernel_one, features.shape)
+    back_one, delta_two = lax.optimization_barrier((back_one, delta_two))
     grad_one, weighted_one = norm_back(
         back_one, centred_one, scaled_one, own(gains[0]), own(scales[0]), members, per
     )

time: 155 us -> 145 us (0.935)
  waiting for transfers between devices: 46.7 us -> 41 us
  starting transfers between devices: 44.9 us -> 39.3 us
  local copies, waits for them, and re-layouts: 18.1 us -> 21 us
    ppermute x9, waiting for transfers between devices: 32.9 us -> 18.3 us  [clip_totals(): lax.ppermute(values, CLIP, [(i, i ^ step) for i in range(count)])]
    all_to_all x1, waiting for transfers between devices: 0.01 us -> 10.4 us  [exchanged(): blocks = lax.all_to_all(fields, CLIP, 0, 0, tiled=True)]
    ppermute x10, waiting for transfers between devices: 12.1 us -> 5.3 us  [moved(): return lax.ppermute(block, CLIP, route)]
    ppermute x9, starting transfers between devices: 20.4 us -> 14.4 us  [clip_totals(): lax.ppermute(values, CLIP, [(i, i ^ step) for i in range(count)])]
    all_gather x1, waiting for transfers between devices: 0.01 us -> 4.89 us  [shards(): grads_one = lax.all_gather(grad_hidden, CLIP)]
    unnamed x8, other arithmetic: 1.9 us -> 0.26 us
    unnamed x73 -> x85, local copies, waits for them, and re-layouts: 7.04 us -> 8.46 us
  transfers between devices with their start and end apart: 24 -> 24, of which waited for: 12 -> 13; matrix products, arithmetic and copies ran while one was open for 19% -> 21% of each run, Pallas kernels for 5% -> 5%
where the time goes in v3:
time: 145 us; the launch traced here: 144 us
  waiting for transfers between devices  41 us (28%)
  starting transfers between devices  39.3 us (27%)
  local copies, waits for them, and re-layouts  21 us (14%)
  between operations  14.7 us (10%)
  Pallas kernels  13.9 us (10%)
  other arithmetic  9.6 us (7%)
  matrix products  4.53 us (3%)
    ppermute x9, waiting for transfers between devices, clip_totals(): lax.ppermute(values, CLIP, [(i, i ^ step) for i in range(count)])  18.3 us
    ppermute x10, starting transfers between devices, moved(): return lax.ppermute(block, CLIP, route)  16.1 us
    ppermute x9, starting transfers between devices, clip_totals(): lax.ppermute(values, CLIP, [(i, i ^ step) for i in range(count)])  14.4 us
    pallas_call x2, Pallas kernels, delta_share(): pl.pallas_call(body, grid=(total,), in_specs=[pl.BlockSpec((1, space, 1,...  13.9 us
    all_to_all x1, waiting for transfers between devices, exchanged(): blocks = lax.all_to_all(fields, CLIP, 0, 0, tiled=True)  10.4 us
    unnamed x85, local copies, waits for them, and re-layouts  8.46 us
    all_to_all x1, starting transfers between devices, exchanged(): blocks = lax.all_to_all(fields, CLIP, 0, 0, tiled=True)  8.42 us
    ppermute x10, waiting for transfers between devices, moved(): return lax.ppermute(block, CLIP, route)  5.3 us
  transfers between devices with their start and end apart: 24, of which 13 were waited for; matrix products, arithmetic and copies ran while one was open for 21% of the time, Pallas kernels for 5%

profile of v3, /device:TPU:0, one launch (start us, length us, event | category | flops | bytes accessed | tf_op | source)
XLA Modules:
  0.0 144.0 jit_solution(2100888077510993630)
XLA Ops:
  7.2 1.1 constant_dynamic-slice_fusion.15
  8.4 1.3 collective-permute-start.6
  9.7 4.9 %collective-permute-start.3 = (bf16[2,1,90,128]{3,2,1,0:T(8,128)(2,1)S(1)}, bf16[2,1,90,128]{3,2,1,0:T(8,128)(2,1)S(1)}, u32[]{:S(2)}, u32[]{:S(2)}) collective-permute-start(bf16[2,1,90,128]{3,2,1,0:T(8,128)(2,1)S(1)} %get-tuple-element.38), channel_id=1, source_target_pairs={{0,2},{4,6},{8,10},{12,14},{1,3},{5,7},{9,11},{13,15},{16,18},{20,... | collective-permute-start | bytes 138248 | tf_op jit(solution)/shard_map/ppermute | solution.py:75
  15.3 1.3 collective-permute-start.4
  16.6 1.1 convert_reduce_fusion.1
  17.7 1.1 convert_reduce_fusion
  18.9 2.7 %collective-permute-start = (f32[4,256]{1,0:T(4,128)S(1)}, f32[4,256]{1,0:T(4,128)S(1)}, u32[]{:S(2)}, u32[]{:S(2)}) collective-permute-start(f32[4,256]{1,0:T(4,128)S(1)} %pad_maximum_fusion.8), channel_id=1, source_target_pairs={{0,2},{2,0},{4,6},{6,4},{8,10},{10,8},{12,14},{14,12},{1,3},{3,1},... | collective-permute-start | bytes 12296 | tf_op jit(solution)/shard_map/ppermute | solution.py:23
  21.6 1.8 %copy_bitcast_fusion = (bf16[1,2,4,90,256]{4,3,2,1,0:T(8,128)(2,1)}, f32[2,4,90,256]{3,2,1,0:T(8,128)S(1)}) fusion(bf16[2,4,90,256]{3,1,2,0:T(4,128)(2,1)} %param.7), kind=kLoop, calls=%fused_computation.26 | loop fusion | flops 184320 | bytes 1474560 | tf_op jit(solution)/shard_map/stack | solution.py:216
  23.4 1.3 fusion.65
  24.8 3.3 %collective-permute-start.1 = (f32[4,256]{1,0:T(4,128)S(1)}, f32[4,256]{1,0:T(4,128)S(1)}, u32[]{:S(2)}, u32[]{:S(2)}) collective-permute-start(f32[4,256]{1,0:T(4,128)S(1)} %fusion.59), channel_id=1, source_target_pairs={{0,4},{2,6},{4,0},{6,2},{8,12},{10,14},{12,8},{14,10},{1,5},{3,7},... | collective-permute-start | bytes 12296 | tf_op jit(solution)/shard_map/ppermute | solution.py:23
  28.1 2.0 %collective-permute-done.1 = f32[4,256]{1,0:T(4,128)S(1)} collective-permute-done((f32[4,256]{1,0:T(4,128)S(1)}, f32[4,256]{1,0:T(4,128)S(1)}, u32[]{:S(2)}, u32[]{:S(2)}) %collective-permute-start.1) | collective-permute-done | bytes 4128 | tf_op jit(solution)/shard_map/ppermute | solution.py:23
  30.1 2.7 %collective-permute-start.2 = (f32[4,256]{1,0:T(4,128)S(1)}, f32[4,256]{1,0:T(4,128)S(1)}, u32[]{:S(2)}, u32[]{:S(2)}) collective-permute-start(f32[4,256]{1,0:T(4,128)S(1)} %fusion.72), channel_id=1, source_target_pairs={{0,8},{2,10},{4,12},{6,14},{8,0},{10,2},{12,4},{14,6},{1,9},{3,11}... | collective-permute-start | bytes 12296 | tf_op jit(solution)/shard_map/ppermute | solution.py:23
  33.3 1.5 %collective-permute-done.2 = f32[4,256]{1,0:T(4,128)S(1)} collective-permute-done((f32[4,256]{1,0:T(4,128)S(1)}, f32[4,256]{1,0:T(4,128)S(1)}, u32[]{:S(2)}, u32[]{:S(2)}) %collective-permute-start.2) | collective-permute-done | bytes 4128 | tf_op jit(solution)/shard_map/ppermute | solution.py:23
  34.9 1.3 collective-permute-start.7
  36.5 5.3 %collective-permute-done.7 = bf16[2,1,90,128]{3,2,1,0:T(8,128)(2,1)S(1)} collective-permute-done((bf16[2,1,90,128]{3,2,1,0:T(8,128)(2,1)S(1)}, bf16[2,1,90,128]{3,2,1,0:T(8,128)(2,1)S(1)}, u32[]{:S(2)}, u32[]{:S(2)}) %collective-permute-start.7) | collective-permute-done | bytes 46112 | tf_op jit(solution)/shard_map/ppermute | solution.py:75
  43.6 1.6 %convolution_bitcast_fusion = f32[2,4,90,256]{3,2,1,0:T(8,128)S(1)} fusion(bf16[2,4,90,27,128]{4,2,3,1,0:T(8,128)(2,1)S(1)} %bitcast_dynamic-update-slice_fusion.38, bf16[256,27,128,1,1]{2,0,1,4,3:T(8,128)(2,1)S(1)} %bitcast.247), kind=kOutput, calls=%fused_computation.6 | convolution fusion | flops 1274019840 | bytes 7483392 | tf_op jit(solution)/shard_map/dot_general | solution.py:187
  45.4 1.7 %collective-permute-done.8 = f32[2,4,90,128]{3,2,1,0:T(8,128)S(1)} collective-permute-done((f32[2,4,90,128]{3,2,1,0:T(8,128)S(1)}, f32[2,4,90,128]{3,2,1,0:T(8,128)S(1)}, u32[]{:S(2)}, u32[]{:S(2)}) %collective-permute-start.8) | collective-permute-done | bytes 368672 | tf_op jit(solution)/shard_map/ppermute | solution.py:177
  47.4 3.7 %collective-permute-done.9 = f32[2,128]{1,0:T(2,128)S(1)} collective-permute-done((f32[2,128]{1,0:T(2,128)S(1)}, f32[2,128]{1,0:T(2,128)S(1)}, u32[]{:S(2)}, u32[]{:S(2)}) %collective-permute-start.9) | collective-permute-done | bytes 1056 | tf_op jit(solution)/shard_map/ppermute | solution.py:23
  51.2 1.5 %collective-permute-start.10 = (f32[2,128]{1,0:T(2,128)S(1)}, f32[2,128]{1,0:T(2,128)S(1)}, u32[]{:S(2)}, u32[]{:S(2)}) collective-permute-start(f32[2,128]{1,0:T(2,128)S(1)} %fusion.58), channel_id=1, source_target_pairs={{0,4},{2,6},{4,0},{6,2},{8,12},{10,14},{12,8},{14,10},{1,5},{3,7},... | collective-permute-start | bytes 3080 | tf_op jit(solution)/shard_map/ppermute | solution.py:23
  52.7 1.0 copy_bitcast_fusion.1
  53.7 1.1 collective-permute-done.10
  54.8 2.5 %collective-permute-start.11 = (f32[2,128]{1,0:T(2,128)S(1)}, f32[2,128]{1,0:T(2,128)S(1)}, u32[]{:S(2)}, u32[]{:S(2)}) collective-permute-start(f32[2,128]{1,0:T(2,128)S(1)} %fusion.71), channel_id=1, source_target_pairs={{0,8},{2,10},{4,12},{6,14},{8,0},{10,2},{12,4},{14,6},{1,9},{3,11}... | collective-permute-start | bytes 3080 | tf_op jit(solution)/shard_map/ppermute | solution.py:23
  57.3 2.1 %collective-permute-done.11 = f32[2,128]{1,0:T(2,128)S(1)} collective-permute-done((f32[2,128]{1,0:T(2,128)S(1)}, f32[2,128]{1,0:T(2,128)S(1)}, u32[]{:S(2)}, u32[]{:S(2)}) %collective-permute-start.11) | collective-permute-done | bytes 1056 | tf_op jit(solution)/shard_map/ppermute | solution.py:23
  60.4 1.3 collective-permute-start.15
  61.7 2.2 %collective-permute-start.12 = (bf16[2,1,90,128]{3,2,1,0:T(8,128)(2,1)S(1)}, bf16[2,1,90,128]{3,2,1,0:T(8,128)(2,1)S(1)}, u32[]{:S(2)}, u32[]{:S(2)}) collective-permute-start(bf16[2,1,90,128]{3,2,1,0:T(8,128)(2,1)S(1)} %get-tuple-element.36), channel_id=1, source_target_pairs={{0,2},{4,6},{8,10},{12,14},{1,3},{5,7},{9,11},{13,15},{16,18},{20,... | collective-permute-start | bytes 138248 | tf_op jit(solution)/shard_map/ppermute | solution.py:75
  64.5 1.3 collective-permute-start.13
  65.8 1.3 collective-permute-start.16
  67.2 1.2 copy.117
  68.4 2.2 %copy.118 = bf16[8,2,2,32,384]{4,3,2,1,0:T(8,128)(2,1)} copy(bf16[8,2,2,32,384]{4,3,0,2,1:T(8,128)(2,1)} %bitcast.253) | data formatting | bytes 1572864 | tf_op jit(solution)/shard_map/transpose | solution.py:92
  70.6 8.4 %all-to-all-start = ((bf16[8,2,2,32,384]{4,3,2,1,0:T(8,128)(2,1)}), bf16[8,2,2,32,384]{4,3,2,1,0:T(8,128)(2,1)}, u32[]{:S(2)}, u32[]{:S(2)}) async-start(bf16[8,2,2,32,384]{4,3,2,1,0:T(8,128)(2,1)} %copy.118), calls=%async_computation | async-start | bytes 1572864 | tf_op jit(solution)/shard_map/all_to_all | solution.py:94
  82.3 1.6 %fusion.4 = f32[2,4,90,256]{3,2,0,1:T(8,128)S(1)} fusion(bf16[256,27,128,1,1]{2,0,3,4,1:T(8,128)(2,1)S(1)} %bitcast.278, bf16[2,4,90,27,128]{4,2,1,0,3:T(8,128)(2,1)S(1)} %bitcast_dynamic-update-slice_fusion.18), kind=kOutput, calls=%fused_computation.5 | convolution fusion | flops 1274019840 | bytes 7483392 | tf_op jit(solution)/shard_map/dot_general | solution.py:187
  85.8 0.8 copy_add_fusion
  86.6 1.7 %copy.121 = bf16[16,4,90,128]{3,2,1,0:T(8,128)(2,1)S(1)} copy(bf16[16,4,90,128]{3,1,2,0:T(4,128)(2,1)} %all-gather.5.cloned.1.call-done) | data formatting | bytes 2949120 | tf_op jit(solution)/shard_map/all_gather | solution.py:215
  88.3 10.4 %all-to-all-done = bf16[8,2,2,32,384]{4,3,2,1,0:T(8,128)(2,1)} async-done(((bf16[8,2,2,32,384]{4,3,2,1,0:T(8,128)(2,1)}), bf16[8,2,2,32,384]{4,3,2,1,0:T(8,128)(2,1)}, u32[]{:S(2)}, u32[]{:S(2)}) %all-to-all-start) | async-done | bytes 786464 | tf_op jit(solution)/shard_map/all_to_all | solution.py:94
  98.7 7.0 %delta_share.2 = f32[32,3,3,3,128]{4,3,2,1,0:T(4,128)S(1)} custom-call(bf16[4,2,2,2,32,384]{5,4,3,2,1,0:T(8,128)(2,1)} %bitcast.106.field_ref, f32[32,3]{1,0:T(8,128)S(1)} %bitcast.251, bf16[8,2,4,90,128]{4,3,2,1,0:T(8,128)(2,1)S(1)} %bitcast.248), custom_call_target="tpu_custom_call" | custom-call | flops 1358954496 | bytes 4194304 | tf_op jit(solution)/shard_map/delta_share/pallas_call | solution.py:149
  105.7 0.8 copy-done.1
  106.5 0.9 fusion.60
  107.4 1.4 collective-permute-start.18
  108.8 2.2 %collective-permute-done.18 = f32[2,128]{1,0:T(2,128)S(1)} collective-permute-done((f32[2,128]{1,0:T(2,128)S(1)}, f32[2,128]{1,0:T(2,128)S(1)}, u32[]{:S(2)}, u32[]{:S(2)}) %collective-permute-start.18) | collective-permute-done | bytes 1056 | tf_op jit(solution)/shard_map/ppermute | solution.py:23
  111.1 3.8 %collective-permute-done.19 = f32[2,128]{1,0:T(2,128)S(1)} collective-permute-done((f32[2,128]{1,0:T(2,128)S(1)}, f32[2,128]{1,0:T(2,128)S(1)}, u32[]{:S(2)}, u32[]{:S(2)}) %collective-permute-start.19) | collective-permute-done | bytes 1056 | tf_op jit(solution)/shard_map/ppermute | solution.py:23
  115.8 1.9 %copy.127 = f32[32,3,3,3,128]{4,0,3,2,1:T(8,128)} copy(f32[32,3,3,3,128]{4,3,2,1,0:T(4,128)} %copy-done.1) | data formatting | bytes 884736
  117.6 1.8 %collective-permute-done.20 = f32[2,128]{1,0:T(2,128)S(1)} collective-permute-done((f32[2,128]{1,0:T(2,128)S(1)}, f32[2,128]{1,0:T(2,128)S(1)}, u32[]{:S(2)}, u32[]{:S(2)}) %collective-permute-start.20) | collective-permute-done | bytes 1056 | tf_op jit(solution)/shard_map/ppermute | solution.py:23
  119.5 0.9 convolution_multiply_fusion.1
  120.3 1.2 add_convert_fusion
  122.8 4.9 %all-gather.7.cloned.1.call-done = bf16[16,4,90,128]{3,1,2,0:T(4,128)(2,1)} async-done(((bf16[2,4,90,128]{3,1,2,0:T(4,128)(2,1)}), bf16[16,4,90,128]{3,1,2,0:T(4,128)(2,1)}) %all-gather.7.cloned.1.call-update) | async-done | bytes 1474576 | tf_op jit(solution)/shard_map/all_gather | solution.py:241
  127.7 1.7 %copy.124 = bf16[16,4,90,128]{3,2,1,0:T(8,128)(2,1)S(1)} copy(bf16[16,4,90,128]{3,1,2,0:T(4,128)(2,1)} %all-gather.7.cloned.1.call-done) | data formatting | bytes 2949120 | tf_op jit(solution)/shard_map/all_gather | solution.py:241
  129.4 6.9 %delta_share.3 = f32[32,3,3,3,128]{4,3,2,1,0:T(4,128)S(1)} custom-call(bf16[4,2,2,2,32,384]{5,4,3,2,1,0:T(8,128)(2,1)} %bitcast.106.field_ref, f32[32,3]{1,0:T(8,128)S(1)} %bitcast.250, bf16[8,2,4,90,128]{4,3,2,1,0:T(8,128)(2,1)S(1)} %bitcast.249), custom_call_target="tpu_custom_call" | custom-call | flops 1358954496 | bytes 4194304 | tf_op jit(solution)/shard_map/delta_share/pallas_call | solution.py:149
  136.3 0.8 copy.126
  (153 shorter events, 12.8 us)
Async XLA Ops:
  7.2 36.4 %copy-start = (bf16[256,3,3,3,128]{4,0,3,2,1:T(8,128)(2,1)S(1)}, bf16[256,3,3,3,128]{4,0,3,2,1:T(8,128)(2,1)}, u32[]{:S(2)}) copy-start(bf16[256,3,3,3,128]{4,0,3,2,1:T(8,128)(2,1)} %param.10) | copy-start | bytes 5308420
  7.2 79.4 %all-gather.5.cloned.1.call-start = ((), (), s32[]{:S(2)}) async-start(), calls=%async_computation.1 | async-start | bytes 1658880 | tf_op jit(solution)/shard_map/all_gather | solution.py:215
  8.3 6.9 %copy-start.2 = (bf16[2,4,90,128]{3,1,2,0:T(4,128)(2,1)}, bf16[2,4,90,128]{3,1,2,0:T(4,128)(2,1)S(1)}, u32[]{:S(2)}) copy-start(bf16[2,4,90,128]{3,1,2,0:T(4,128)(2,1)S(1)} %constant_dynamic-slice_fusion.15) | copy-start | bytes 552964
  8.4 33.4 %collective-permute-start.6 = (bf16[2,4,90,128]{3,2,1,0:T(8,128)(2,1)S(1)}, bf16[2,4,90,128]{3,2,1,0:T(8,128)(2,1)S(1)}, u32[]{:S(2)}, u32[]{:S(2)}) collective-permute-start(bf16[2,4,90,128]{3,2,1,0:T(8,128)(2,1)S(1)} %copy.131), channel_id=1, source_target_pairs={{4,0},{6,2},{8,4},{10,6},{12,8},{14,10},{5,1},{7,3},{9,5},{11,7},{... | collective-permute-start | bytes 552968 | tf_op jit(solution)/shard_map/ppermute | solution.py:75
  9.7 26.7 %collective-permute-start.3 = (bf16[2,1,90,128]{3,2,1,0:T(8,128)(2,1)S(1)}, bf16[2,1,90,128]{3,2,1,0:T(8,128)(2,1)S(1)}, u32[]{:S(2)}, u32[]{:S(2)}) collective-permute-start(bf16[2,1,90,128]{3,2,1,0:T(8,128)(2,1)S(1)} %get-tuple-element.38), channel_id=1, source_target_pairs={{0,2},{4,6},{8,10},{12,14},{1,3},{5,7},{9,11},{13,15},{16,18},{20,... | collective-permute-start | bytes 138248 | tf_op jit(solution)/shard_map/ppermute | solution.py:75
  14.6 21.9 %collective-permute-start.5 = (bf16[2,1,90,128]{3,2,1,0:T(8,128)(2,1)S(1)}, bf16[2,1,90,128]{3,2,1,0:T(8,128)(2,1)S(1)}, u32[]{:S(2)}, u32[]{:S(2)}) collective-permute-start(bf16[2,1,90,128]{3,2,1,0:T(8,128)(2,1)S(1)} %get-tuple-element.38), channel_id=1, source_target_pairs={{4,2},{8,6},{12,10},{5,3},{9,7},{13,11},{20,18},{24,22},{28,26},{2... | collective-permute-start | bytes 138248 | tf_op jit(solution)/shard_map/ppermute | solution.py:75
  15.3 21.2 %collective-permute-start.4 = (bf16[2,1,90,128]{3,2,1,0:T(8,128)(2,1)S(1)}, bf16[2,1,90,128]{3,2,1,0:T(8,128)(2,1)S(1)}, u32[]{:S(2)}, u32[]{:S(2)}) collective-permute-start(bf16[2,1,90,128]{3,2,1,0:T(8,128)(2,1)S(1)} %get-tuple-element.39), channel_id=1, source_target_pairs={{2,0},{6,4},{10,8},{14,12},{3,1},{7,5},{11,9},{15,13},{18,16},{22,... | collective-permute-start | bytes 138248 | tf_op jit(solution)/shard_map/ppermute | solution.py:75
  18.9 5.9 %collective-permute-start = (f32[4,256]{1,0:T(4,128)S(1)}, f32[4,256]{1,0:T(4,128)S(1)}, u32[]{:S(2)}, u32[]{:S(2)}) collective-permute-start(f32[4,256]{1,0:T(4,128)S(1)} %pad_maximum_fusion.8), channel_id=1, source_target_pairs={{0,2},{2,0},{4,6},{6,4},{8,10},{10,8},{12,14},{14,12},{1,3},{3,1},... | collective-permute-start | bytes 12296 | tf_op jit(solution)/shard_map/ppermute | solution.py:23
  24.8 8.1 %copy-start.11 = (f32[1,256]{1,0:T(1,128)}, f32[1,256]{1,0:T(1,128)S(1)}, u32[]{:S(2)}) copy-start(f32[1,256]{1,0:T(1,128)S(1)} %get-tuple-element.43) | copy-start | bytes 3076
  24.8 5.3 %collective-permute-start.1 = (f32[4,256]{1,0:T(4,128)S(1)}, f32[4,256]{1,0:T(4,128)S(1)}, u32[]{:S(2)}, u32[]{:S(2)}) collective-permute-start(f32[4,256]{1,0:T(4,128)S(1)} %fusion.59), channel_id=1, source_target_pairs={{0,4},{2,6},{4,0},{6,2},{8,12},{10,14},{12,8},{14,10},{1,5},{3,7},... | collective-permute-start | bytes 12296 | tf_op jit(solution)/shard_map/ppermute | solution.py:23
  30.1 4.8 %collective-permute-start.2 = (f32[4,256]{1,0:T(4,128)S(1)}, f32[4,256]{1,0:T(4,128)S(1)}, u32[]{:S(2)}, u32[]{:S(2)}) collective-permute-start(f32[4,256]{1,0:T(4,128)S(1)} %fusion.72), channel_id=1, source_target_pairs={{0,8},{2,10},{4,12},{6,14},{8,0},{10,2},{12,4},{14,6},{1,9},{3,11}... | collective-permute-start | bytes 12296 | tf_op jit(solution)/shard_map/ppermute | solution.py:23
  34.9 6.9 %collective-permute-start.7 = (bf16[2,1,90,128]{3,2,1,0:T(8,128)(2,1)S(1)}, bf16[2,1,90,128]{3,2,1,0:T(8,128)(2,1)S(1)}, u32[]{:S(2)}, u32[]{:S(2)}) collective-permute-start(bf16[2,1,90,128]{3,2,1,0:T(8,128)(2,1)S(1)} %get-tuple-element.39), channel_id=1, source_target_pairs={{6,0},{10,4},{14,8},{7,1},{11,5},{15,9},{22,16},{26,20},{30,24},{2... | collective-permute-start | bytes 138248 | tf_op jit(solution)/shard_map/ppermute | solution.py:75
  42.2 1.1 copy-start.3
  43.6 3.5 %copy-start.13 = (f32[128]{0:T(128)S(1)}, f32[128]{0:T(128)}, u32[]{:S(2)}) copy-start(f32[128]{0:T(128)} %fusion.52) | copy-start | bytes 1540
  43.6 9.0 %copy-start.7 = (bf16[2,4,90,256]{3,1,2,0:T(4,128)(2,1)S(1)}, bf16[2,4,90,256]{3,1,2,0:T(4,128)(2,1)}, u32[]{:S(2)}) copy-start(bf16[2,4,90,256]{3,1,2,0:T(4,128)(2,1)} %param.6) | copy-start | bytes 1105924
  43.6 23.5 %copy-start.5 = (bf16[1,2,4,90,256]{4,3,2,1,0:T(8,128)(2,1)S(1)}, bf16[1,2,4,90,256]{4,3,2,1,0:T(8,128)(2,1)}, u32[]{:S(2)}) copy-start(bf16[1,2,4,90,256]{4,3,2,1,0:T(8,128)(2,1)} %get-tuple-element.34) | copy-start | bytes 1105924
  45.3 1.8 %collective-permute-start.8 = (f32[2,4,90,128]{3,2,1,0:T(8,128)S(1)}, f32[2,4,90,128]{3,2,1,0:T(8,128)S(1)}, u32[]{:S(2)}, u32[]{:S(2)}) collective-permute-start(f32[2,4,90,128]{3,2,1,0:T(8,128)S(1)} %constant_dynamic-slice_fusion.12), channel_id=1, source_target_pairs={{0,1},{1,0},{2,3},{3,2},{4,5},{5,4},{6,7},{7,6},{8,9},{9,8},{10,11... | collective-permute-start | bytes 1105928 | tf_op jit(solution)/shard_map/ppermute | solution.py:177
  47.4 3.8 %collective-permute-start.9 = (f32[2,128]{1,0:T(2,128)S(1)}, f32[2,128]{1,0:T(2,128)S(1)}, u32[]{:S(2)}, u32[]{:S(2)}) collective-permute-start(f32[2,128]{1,0:T(2,128)S(1)} %pad_maximum_fusion.9), channel_id=1, source_target_pairs={{0,2},{2,0},{4,6},{6,4},{8,10},{10,8},{12,14},{14,12},{1,3},{3,1},... | collective-permute-start | bytes 3080 | tf_op jit(solution)/shard_map/ppermute | solution.py:23
  51.2 3.6 %collective-permute-start.10 = (f32[2,128]{1,0:T(2,128)S(1)}, f32[2,128]{1,0:T(2,128)S(1)}, u32[]{:S(2)}, u32[]{:S(2)}) collective-permute-start(f32[2,128]{1,0:T(2,128)S(1)} %fusion.58), channel_id=1, source_target_pairs={{0,4},{2,6},{4,0},{6,2},{8,12},{10,14},{12,8},{14,10},{1,5},{3,7},... | collective-permute-start | bytes 3080 | tf_op jit(solution)/shard_map/ppermute | solution.py:23
  54.8 4.6 %collective-permute-start.11 = (f32[2,128]{1,0:T(2,128)S(1)}, f32[2,128]{1,0:T(2,128)S(1)}, u32[]{:S(2)}, u32[]{:S(2)}) collective-permute-start(f32[2,128]{1,0:T(2,128)S(1)} %fusion.71), channel_id=1, source_target_pairs={{0,8},{2,10},{4,12},{6,14},{8,0},{10,2},{12,4},{14,6},{1,9},{3,11}... | collective-permute-start | bytes 3080 | tf_op jit(solution)/shard_map/ppermute | solution.py:23
  57.3 2.9 %copy-start.16 = (s32[128]{0:T(128)}, s32[128]{0:T(128)S(1)}, u32[]{:S(2)}) copy-start(s32[128]{0:T(128)S(1)} %and_select_fusion) | copy-start | bytes 1540
  59.5 0.6 copy-start.14
  60.4 19.7 %collective-permute-start.15 = (bf16[2,4,90,128]{3,2,1,0:T(8,128)(2,1)S(1)}, bf16[2,4,90,128]{3,2,1,0:T(8,128)(2,1)S(1)}, u32[]{:S(2)}, u32[]{:S(2)}) collective-permute-start(bf16[2,4,90,128]{3,2,1,0:T(8,128)(2,1)S(1)} %multiply_convert_fusion), channel_id=1, source_target_pairs={{4,0},{6,2},{8,4},{10,6},{12,8},{14,10},{5,1},{7,3},{9,5},{11,7},{... | collective-permute-start | bytes 552968 | tf_op jit(solution)/shard_map/ppermute | solution.py:75
  61.7 18.3 %collective-permute-start.12 = (bf16[2,1,90,128]{3,2,1,0:T(8,128)(2,1)S(1)}, bf16[2,1,90,128]{3,2,1,0:T(8,128)(2,1)S(1)}, u32[]{:S(2)}, u32[]{:S(2)}) collective-permute-start(bf16[2,1,90,128]{3,2,1,0:T(8,128)(2,1)S(1)} %get-tuple-element.36), channel_id=1, source_target_pairs={{0,2},{4,6},{8,10},{12,14},{1,3},{5,7},{9,11},{13,15},{16,18},{20,... | collective-permute-start | bytes 138248 | tf_op jit(solution)/shard_map/ppermute | solution.py:75
  63.9 16.2 %collective-permute-start.14 = (bf16[2,1,90,128]{3,2,1,0:T(8,128)(2,1)S(1)}, bf16[2,1,90,128]{3,2,1,0:T(8,128)(2,1)S(1)}, u32[]{:S(2)}, u32[]{:S(2)}) collective-permute-start(bf16[2,1,90,128]{3,2,1,0:T(8,128)(2,1)S(1)} %get-tuple-element.36), channel_id=1, source_target_pairs={{4,2},{8,6},{12,10},{5,3},{9,7},{13,11},{20,18},{24,22},{28,26},{2... | collective-permute-start | bytes 138248 | tf_op jit(solution)/shard_map/ppermute | solution.py:75
  64.5 15.5 %collective-permute-start.13 = (bf16[2,1,90,128]{3,2,1,0:T(8,128)(2,1)S(1)}, bf16[2,1,90,128]{3,2,1,0:T(8,128)(2,1)S(1)}, u32[]{:S(2)}, u32[]{:S(2)}) collective-permute-start(bf16[2,1,90,128]{3,2,1,0:T(8,128)(2,1)S(1)} %get-tuple-element.37), channel_id=1, source_target_pairs={{2,0},{6,4},{10,8},{14,12},{3,1},{7,5},{11,9},{15,13},{18,16},{22,... | collective-permute-start | bytes 138248 | tf_op jit(solution)/shard_map/ppermute | solution.py:75
  65.8 14.2 %collective-permute-start.16 = (bf16[2,1,90,128]{3,2,1,0:T(8,128)(2,1)S(1)}, bf16[2,1,90,128]{3,2,1,0:T(8,128)(2,1)S(1)}, u32[]{:S(2)}, u32[]{:S(2)}) collective-permute-start(bf16[2,1,90,128]{3,2,1,0:T(8,128)(2,1)S(1)} %get-tuple-element.37), channel_id=1, source_target_pairs={{6,0},{10,4},{14,8},{7,1},{11,5},{15,9},{22,16},{26,20},{30,24},{2... | collective-permute-start | bytes 138248 | tf_op jit(solution)/shard_map/ppermute | solution.py:75
  70.6 28.1 %all-to-all-start = ((bf16[8,2,2,32,384]{4,3,2,1,0:T(8,128)(2,1)}), bf16[8,2,2,32,384]{4,3,2,1,0:T(8,128)(2,1)}, u32[]{:S(2)}, u32[]{:S(2)}) async-start(bf16[8,2,2,32,384]{4,3,2,1,0:T(8,128)(2,1)} %copy.118), calls=%async_computation | async-start | bytes 1572864 | tf_op jit(solution)/shard_map/all_to_all | solution.py:94
  79.0 48.7 %all-gather.7.cloned.1.call-start = ((), (), s32[]{:S(2)}) async-start(), calls=%async_computation.2 | async-start | bytes 1658880 | tf_op jit(solution)/shard_map/all_gather | solution.py:241
  80.8 1.5 %copy-start.15 = (bf16[256,3,3,3,128]{4,0,3,2,1:T(8,128)(2,1)S(1)}, bf16[256,3,3,3,128]{4,0,3,2,1:T(8,128)(2,1)}, u32[]{:S(2)}) copy-start(bf16[256,3,3,3,128]{4,0,3,2,1:T(8,128)(2,1)} %param.9) | copy-start | bytes 5308420
  82.3 1.8 %copy-start.10 = (f32[1,256]{1,0:T(1,128)S(1)}, f32[1,256]{1,0:T(1,128)}, u32[]{:S(2)}) copy-start(f32[1,256]{1,0:T(1,128)} %get-tuple-element.42) | copy-start | bytes 3076
  82.3 2.4 %copy-start.12 = (f32[1,256]{1,0:T(1,128)S(1)}, f32[1,256]{1,0:T(1,128)}, u32[]{:S(2)}) copy-start(f32[1,256]{1,0:T(1,128)} %copy-done.11) | copy-start | bytes 3076
  84.0 1.8 %collective-permute-start.17 = (f32[2,4,90,128]{3,2,1,0:T(8,128)S(1)}, f32[2,4,90,128]{3,2,1,0:T(8,128)S(1)}, u32[]{:S(2)}, u32[]{:S(2)}) collective-permute-start(f32[2,4,90,128]{3,2,1,0:T(8,128)S(1)} %copy.133), channel_id=1, source_target_pairs={{0,1},{1,0},{2,3},{3,2},{4,5},{5,4},{6,7},{7,6},{8,9},{9,8},{10,11... | collective-permute-start | bytes 1105928 | tf_op jit(solution)/shard_map/ppermute | solution.py:177
  85.4 21.1 %copy-start.8 = (f32[128]{0:T(128)S(1)}, f32[128]{0:T(128)}, u32[]{:S(2)}) copy-start(f32[128]{0:T(128)} %get-tuple-element.52) | copy-start | bytes 1540
  85.4 21.1 %copy-start.9 = (f32[128]{0:T(128)S(1)}, f32[128]{0:T(128)}, u32[]{:S(2)}) copy-start(f32[128]{0:T(128)} %get-tuple-element.53) | copy-start | bytes 1540
  98.7 7.8 %copy-start.4 = (f32[2,4,90,256]{3,2,1,0:T(8,128)S(1)}, f32[2,4,90,256]{3,2,1,0:T(8,128)}, u32[]{:S(2)}) copy-start(f32[2,4,90,256]{3,2,1,0:T(8,128)} %get-tuple-element.33) | copy-start | bytes 2211844
  98.7 7.8 %copy-start.6 = (f32[2,4,90,128]{3,2,1,0:T(8,128)S(1)}, f32[2,4,90,128]{3,2,1,0:T(8,128)}, u32[]{:S(2)}) copy-start(f32[2,4,90,128]{3,2,1,0:T(8,128)} %copy_add_fusion) | copy-start | bytes 1105924
  105.7 0.8 copy-start.1
  107.4 3.6 %collective-permute-start.18 = (f32[2,128]{1,0:T(2,128)S(1)}, f32[2,128]{1,0:T(2,128)S(1)}, u32[]{:S(2)}, u32[]{:S(2)}) collective-permute-start(f32[2,128]{1,0:T(2,128)S(1)} %pad_maximum_fusion.10), channel_id=1, source_target_pairs={{0,2},{2,0},{4,6},{6,4},{8,10},{10,8},{12,14},{14,12},{1,3},{3,1},... | collective-permute-start | bytes 3080 | tf_op jit(solution)/shard_map/ppermute | solution.py:23
  111.0 3.9 %collective-permute-start.19 = (f32[2,128]{1,0:T(2,128)S(1)}, f32[2,128]{1,0:T(2,128)S(1)}, u32[]{:S(2)}, u32[]{:S(2)}) collective-permute-start(f32[2,128]{1,0:T(2,128)S(1)} %fusion.57), channel_id=1, source_target_pairs={{0,4},{2,6},{4,0},{6,2},{8,12},{10,14},{12,8},{14,10},{1,5},{3,7},... | collective-permute-start | bytes 3080 | tf_op jit(solution)/shard_map/ppermute | solution.py:23
  114.9 4.5 %collective-permute-start.20 = (f32[2,128]{1,0:T(2,128)S(1)}, f32[2,128]{1,0:T(2,128)S(1)}, u32[]{:S(2)}, u32[]{:S(2)}) collective-permute-start(f32[2,128]{1,0:T(2,128)S(1)} %fusion.70), channel_id=1, source_target_pairs={{0,8},{2,10},{4,12},{6,14},{8,0},{10,2},{12,4},{14,6},{1,9},{3,11}... | collective-permute-start | bytes 3080 | tf_op jit(solution)/shard_map/ppermute | solution.py:23
Sparse Core Ops, SparseCore 0:
  15.4 45.4 all-gather.4
  82.5 45.1 all-gather.6
